TPU v7x, 128 devices: a whole 4x4x4 slice. The times are simulated.
128 devices in a mesh: dp: 4 (over z), label: 32 (over y, x, core).
Axes of the slice: x: 4, y: 4, z: 4, core: 2. Of those that a mesh axis runs over, the one named last changes fastest.
Arguments:
- queries: bfloat16 [32768, 768], P(('dp', 'label')), may hold values from -6 to 6
- labels: bfloat16 [128, 512, 768], P('label'), may hold values from -0.21875 to 0.21875
- matcher: bfloat16 [128, 768], replicated, may hold values from -0.15 to 0.15
- cluster_ids: int32 [32768, 16], P('dp'), may hold values from 0 to 127, all different within a row; in each aligned block of 256 rows (0 to 255, 256 to 511, ...) at most 48 rows name the same one
- positives: int32 [32768], P('dp'), may hold values from 0 to 8191
Outputs:
- losses: float32 [32768], P(('dp', 'label'))
- query_grads: float32 [32768, 768], P(('dp', 'label'))
- label_grads: float32 [128, 512, 768], P('label', 'dp')
- matcher_grads: float32 [128, 768], replicated
Inputs may be any that keep to these rules, and one draw needn't show every extreme that they name: `cluster_ids`: each row names 16 different leaf clusters; among the 256 rows of one device no cluster is named more than 48 times, and in every draw some device's rows name some cluster exactly 48 times.
All inputs are finite; a program needn't handle non-finite values.
Results may differ from a plain program's by a relative error of at most 0.0095.
Values may be sent and summed in bfloat16 or wider, within the bound.
A program may use at most 128 MiB of HBM per device.

v0:
```python
import jax
import jax.numpy as jnp
from jax import lax
from jax.sharding import PartitionSpec as P

LEAF = 512
K = 16


BIG = 1e30


def in_one_piece(arrays, axis, split_dim, concat_dim, along):
    widths = [a.shape[along] for a in arrays]
    both = jnp.concatenate(arrays, axis=along)
    filled = lax.all_to_all(both, axis, split_axis=split_dim, concat_axis=concat_dim, tiled=True)
    return tuple(jnp.split(filled, [sum(widths[:k]) for k in range(1, len(widths))], axis=along))


def sent_to_all(shard, axis):
    devices = lax.axis_size(axis)
    return lax.all_to_all(
        jnp.broadcast_to(shard[None], (devices, *shard.shape)), axis, 0, 0, tiled=True
    )


def over_copies(shard, axis):
    return sent_to_all(shard, axis).sum(axis=0)


def earlier_counts(named):
    count = named.shape[-2]
    iota = jnp.arange(count, dtype=jnp.int32)
    lower = (iota[:, None] > iota[None, :]).astype(jnp.bfloat16)
    return jnp.einsum(
        "ij,sjc->sic", lower, named.astype(jnp.bfloat16), preferred_element_type=jnp.float32
    )


def body(queries, labels, matcher, cluster_ids, positives):
    q_dev, width = queries.shape
    cl_dev = labels.shape[0]
    clusters = matcher.shape[0]
    n_label = lax.axis_size("label")
    capacity = q_dev * K * 3 // (2 * clusters)
    rows_dev = n_label * capacity
    me = lax.axis_index("label")
    first = me * cl_dev
    slot_iota = jnp.arange(capacity, dtype=jnp.float32)
    shortlist_iota = jnp.arange(K, dtype=jnp.int32)
    own_ids = lax.dynamic_slice_in_dim(cluster_ids, me * q_dev, q_dev, 0)
    all_iota = jnp.arange(clusters, dtype=jnp.int32)
    named_own = jnp.any(own_ids[:, :, None] == all_iota[None, None, :], axis=1)
    rank_own = earlier_counts(named_own[None])[0]
    select_own = named_own.T[:, None, :] & (rank_own.T[:, None, :] == slot_iota[None, :, None])
    select_own = select_own.reshape(n_label, cl_dev, capacity, q_dev).transpose(1, 0, 2, 3)
    select_num = select_own.astype(jnp.bfloat16)
    group_ids = cluster_ids.reshape(n_label, q_dev, K) - first
    group_pos = positives.reshape(n_label, q_dev)
    local_iota = jnp.arange(cl_dev, dtype=jnp.int32)
    named_recv = jnp.any(group_ids[:, :, :, None] == local_iota[None, None, None, :], axis=2)
    rank_recv = earlier_counts(named_recv)
    named_t = named_recv.transpose(2, 0, 1)
    rank_t = rank_recv.transpose(2, 0, 1)
    select_recv = named_t[:, :, None, :] & (rank_t[:, :, None, :] == slot_iota[None, None, :, None])
    pos_slot = group_pos // LEAF
    pos_cluster = jnp.sum(
        jnp.where(shortlist_iota[None, None, :] == pos_slot[:, :, None], group_ids, 0), axis=2
    )
    target_val = jnp.where(
        pos_cluster[None, :, :] == local_iota[:, None, None], (group_pos % LEAF)[None, :, :], -1
    )
    target_map = jnp.sum(jnp.where(select_recv, target_val[:, :, None, :] + 1, 0), axis=3) - 1
    group = lax.all_gather(queries, "label", axis=0, tiled=True).reshape(n_label, q_dev, width)
    picked_rows = jnp.einsum(
        "csri,sid->csrd",
        select_recv.astype(jnp.bfloat16),
        group,
        preferred_element_type=jnp.float32,
    )
    received = picked_rows.astype(jnp.bfloat16).reshape(cl_dev, rows_dev, width)
    match_own = lax.dynamic_slice_in_dim(matcher, first, cl_dev, 0)
    scores = jnp.einsum("csd,cld->csl", received, labels, preferred_element_type=jnp.float32)
    bias = jnp.einsum("csd,cd->cs", received, match_own, preferred_element_type=jnp.float32)
    scores = scores + bias[:, :, None]
    leaf_iota = jnp.arange(LEAF, dtype=jnp.int32)
    hit = (leaf_iota[None, None, :] == target_map.reshape(cl_dev, rows_dev)[:, :, None]).astype(
        jnp.float32
    )
    top = jnp.max(scores, axis=2)
    total = jnp.sum(jnp.exp(scores - top[:, :, None]), axis=2)
    picked = jnp.sum(scores * hit, axis=2)
    shape3 = (cl_dev, n_label, capacity)
    back_top, back_total, back_picked = in_one_piece(
        (top.reshape(shape3), total.reshape(shape3), picked.reshape(shape3)), "label", 1, 1, 0
    )
    best = jnp.max(jnp.where(select_own, back_top[..., None], -BIG), axis=(0, 1, 2))
    spread = jnp.where(
        select_own,
        back_total[..., None] * jnp.exp(back_top[..., None] - best[None, None, None, :]),
        0.0,
    )
    lse = best + jnp.log(jnp.sum(spread, axis=(0, 1, 2)))
    losses = lse - jnp.sum(jnp.where(select_own, back_picked[..., None], 0.0), axis=(0, 1, 2))
    used = jnp.any(select_own, axis=3)
    outgoing_lse = jnp.where(
        used, jnp.sum(jnp.where(select_own, lse[None, None, None, :], 0.0), axis=3), BIG
    )
    slot_lse = lax.all_to_all(
        outgoing_lse, "label", split_axis=1, concat_axis=1, tiled=True
    ).reshape(cl_dev, rows_dev)
    delta = jnp.exp(scores - slot_lse[:, :, None]) - hit
    coef = jnp.sum(delta, axis=2)
    delta_b = delta.astype(jnp.bfloat16)
    coef_b = coef.astype(jnp.bfloat16)
    slot_grad = jnp.einsum("csl,cld->csd", delta_b, labels, preferred_element_type=jnp.float32)
    slot_grad = (
        slot_grad
        + coef_b.astype(jnp.float32)[:, :, None] * match_own.astype(jnp.float32)[:, None, :]
    )
    slot_grad = slot_grad.astype(jnp.bfloat16).reshape(cl_dev, n_label, capacity, width)
    returned = lax.all_to_all(slot_grad, "label", split_axis=1, concat_axis=1, tiled=True)
    query_grads = jnp.einsum(
        "cori,cord->id", select_num, returned, preferred_element_type=jnp.float32
    )
    label_part = jnp.einsum("csl,csd->cld", delta_b, received, preferred_element_type=jnp.float32)
    label_grads = lax.psum_scatter(
        label_part.astype(jnp.bfloat16), "dp", scatter_dimension=1, tiled=True
    ).astype(jnp.float32)
    local_sum = jnp.einsum("cs,csd->cd", coef_b, received, preferred_element_type=jnp.float32)
    local_sum = over_copies(local_sum, "dp")
    matcher_grads = lax.all_gather(local_sum, "label", axis=0, tiled=True)
    return (losses, query_grads, label_grads, matcher_grads)


def solution(mesh):
    return jax.shard_map(
        body,
        mesh=mesh,
        in_specs=(P(("dp", "label"), None), P("label", None, None), P(), P("dp", None), P("dp")),
        out_specs=(P(("dp", "label")), P(("dp", "label"), None), P("label", "dp", None), P()),
        check_vma=False,
    )
```

profile of v0, /device:TPU:1, one launch (start us, length us, event | category | flops | bytes accessed | tf_op | source)
XLA Modules:
  0.0 354.9 jit_solution(14381082785426550311)
XLA Ops:
  7.2 0.0 copy-start
  7.2 0.0 all-gather.3.cloned.1.call-start
  7.2 0.7 all-gather.3.cloned.1.call-update
  7.9 1.6 reshape.137
  9.5 0.7 constant_dynamic-slice_fusion
  10.2 0.1 copy.86
  10.3 1.6 fusion.13
  11.9 0.1 copy.87
  12.1 0.8 add_select_fusion.1
  12.9 1.9 select_reduce_fusion.6
  14.8 0.6 eq.121
  15.4 1.1 copy.130
  16.5 0.5 fusion.14
  17.0 0.2 convolution_bitcast_fusion
  17.2 0.1 copy.92
  17.3 0.8 add_select_fusion
  18.0 0.8 select_add_fusion
  18.9 2.3 select_reduce_fusion.5
  21.2 0.1 sub.68
  21.3 0.0 copy-start.2
  21.3 1.3 dynamic-slice_convert_fusion
  22.6 0.2 convolution_bitcast_fusion.1
  22.8 53.8 %all-gather.3.cloned.1.call-done = bf16[8192,768]{1,0:T(8,128)(2,1)} async-done(((bf16[256,768]{1,0:T(8,128)(2,1)}), bf16[8192,768]{1,0:T(8,128)(2,1)}) %all-gather.3.cloned.1.call-update) | async-done | bytes 12582928 | tf_op jit(solution)/shard_map/all_gather | solution.py:74
  76.6 10.8 %convert_bitcast_fusion = bf16[4,32,48,768]{3,2,0,1:T(8,128)(2,1)} fusion(bf16[32,256,768,1]{2,1,3,0:T(8,128)(2,1)} %bitcast.59, f32[4,32,256]{2,0,1:T(4,128)S(1)} %copy.92, pred[4,32,256]{2,0,1:T(4,128)(4,1)S(1)} %bitcast.66), kind=kOutput, calls=%fused_computation.8 | convolution fusion | flops 2423783424 | bytes 22183936 | tf_op jit(solution)/shard_map/csri,sid->csrd/dot_general | solution.py:75
  87.4 8.1 %copy.93 = bf16[4,32,48,768]{3,2,1,0:T(8,128)(2,1)} copy(bf16[4,32,48,768]{3,2,0,1:T(8,128)(2,1)} %convert_bitcast_fusion) | data formatting | bytes 18874368 | tf_op jit(solution)/shard_map/convert_element_type | solution.py:81
  95.5 6.2 %fusion.30 = f32[4,1,1536]{2,1,0:T(1,128)S(1)} fusion(bf16[4,1536,768]{2,1,0:T(8,128)(2,1)} %bitcast.55, bf16[4,768,1]{1,0,2:T(4,128)(2,1)S(1)} %get-tuple-element.14), kind=kOutput, calls=%fused_computation.61 | convolution fusion | flops 9437184 | bytes 9467904 | tf_op jit(solution)/shard_map/csd,cd->cs/dot_general | solution.py:84
  101.8 11.7 %add_reduce_fusion = (f32[4,1536]{1,0:T(4,128)S(1)}, f32[4,1536,512]{1,2,0:T(8,128)}) fusion(f32[4,1536]{1,0:T(4,128)S(1)} %bitcast.69, bf16[4,1536,768]{2,1,0:T(8,128)(2,1)} %bitcast.56, bf16[4,512,768]{2,1,0:T(8,128)(2,1)S(1)} %copy-done), kind=kOutput, calls=%fused_computation.5 | convolution fusion | flops 4838123520 | bytes 25214976 | tf_op jit(solution)/shard_map/csd,cld->csl/dot_general | solution.py:83
  113.5 0.1 reshape.135
  113.6 7.6 %exponential_reduce_fusion = (f32[4,1536]{1,0:T(4,128)S(1)}, f32[4,1536]{1,0:T(4,128)}) fusion(f32[4,1536,512]{1,2,0:T(8,128)} %get-tuple-element.16, f32[4,1536]{1,0:T(4,128)S(1)} %get-tuple-element.15, f32[4,1536]{1,0:T(4,128)S(1)} %bitcast.70, s32[4,1536]{1,0:T(4,128)S(1)} %sub.68), kind=kLoop, calls=%fused_computation.4 | loop fusion | flops 18862080 | bytes 12705792 | tf_op jit(solution)/shard_map/reduce_sum | solution.py:91
  121.2 0.1 reshape.136
  121.3 0.8 reshape.138
  122.2 0.8 copy.133
  123.0 1.8 reshape.149
  124.8 5.4 %all-to-all-start = ((f32[32,1,576]{2,1,0:T(1,128)}), f32[32,1,576]{2,1,0:T(1,128)S(1)}, u32[]{:S(2)}, u32[]{:S(2)}) async-start(f32[32,1,576]{2,1,0:T(1,128)} %reshape.149), calls=%async_computation | async-start | bytes 163840 | tf_op jit(solution)/shard_map/all_to_all | solution.py:16
  130.2 2.3 fusion.6
  132.5 5.1 %all-to-all-done = f32[32,1,576]{2,1,0:T(1,128)S(1)} async-done(((f32[32,1,576]{2,1,0:T(1,128)}), f32[32,1,576]{2,1,0:T(1,128)S(1)}, u32[]{:S(2)}, u32[]{:S(2)}) %all-to-all-start) | async-done | bytes 73760 | tf_op jit(solution)/shard_map/all_to_all | solution.py:16
  137.6 0.5 broadcast.125
  138.1 0.8 reduce.1
  138.9 0.8 reshape.150
  139.8 1.1 fusion.34
  140.9 1.7 select_reduce_fusion.4
  142.6 2.4 select_reduce_fusion.3
  145.1 3.4 select_reduce_fusion.1
  148.5 0.1 reshape.151
  148.7 10.8 %all_to_all.20 = f32[32,1,192]{2,1,0:T(1,128)S(1)} all-to-all(f32[32,1,192]{2,1,0:T(1,128)S(1)} %reshape.151), channel_id=1, replica_groups=mesh['dp'=4,'label'=32] {'label'}, dimensions={0} | all-to-all | bytes 49152 | tf_op jit(solution)/shard_map/all_to_all | solution.py:109
  159.5 0.7 reduce.2
  160.2 0.1 reshape.152
  160.3 0.1 sub.72
  160.4 0.0 copy-start.3
  160.5 7.7 %fusion.2 = bf16[4,1536]{1,0:T(4,128)(2,1)S(1)} fusion(f32[4,1536,512]{1,2,0:T(8,128)} %get-tuple-element.16, f32[4,1536]{1,0:T(4,128)S(1)} %sub.72, s32[4,1536]{1,0:T(4,128)} %copy-done.2, f32[4,1536]{1,0:T(4,128)S(1)} %bitcast.71), kind=kLoop, calls=%fused_computation.9 | loop fusion | flops 18868224 | bytes 12668928 | tf_op jit(solution)/shard_map/reduce_sum | solution.py:113
  168.2 5.0 %fusion.28 = f32[4,1,768]{2,1,0:T(1,128)S(1)} fusion(bf16[4,1536,768]{2,1,0:T(8,128)(2,1)} %bitcast.57, bf16[4,1536,1]{1,0,2:T(4,128)(2,1)S(1)} %bitcast.74), kind=kOutput, calls=%fused_computation.57 | convolution fusion | flops 9437184 | bytes 9461760 | tf_op jit(solution)/shard_map/cs,csd->cd/dot_general | solution.py:130
  173.2 0.6 broadcast_in_dim.113
  173.8 4.1 %all-to-all-start.3 = ((f32[4,4,768]{2,1,0:T(4,128)}), f32[4,4,768]{2,1,0:T(4,128)S(1)}, u32[]{:S(2)}, u32[]{:S(2)}) async-start(f32[4,4,768]{2,1,0:T(4,128)} %broadcast_in_dim.113), calls=%async_computation.4 | async-start | bytes 98304 | tf_op jit(solution)/shard_map/all_to_all | solution.py:22
  178.0 12.4 %add_convert_fusion = bf16[4,1536,768]{2,1,0:T(8,128)(2,1)} fusion(f32[4,768]{1,0:T(4,128)S(1)} %copy-done.4, f32[4,1536]{1,0:T(4,128)S(1)} %convert_element_type.71, bf16[4,512,768]{2,1,0:T(8,128)(2,1)S(1)} %copy-done, f32[4,1536,512]{1,2,0:T(8,128)} %get-tuple-element.16, f32[4,1536]{1,0:T(4,128)S(1)} %sub.72, s32[4,1536]{1,0:T(4,128)S(1)} %copy-done.3, ...), kind=kOutput, calls=%fused_computation | convolution fusion | flops 4864868352 | bytes 25276416 | tf_op jit(solution)/shard_map/csl,cld->csd/dot_general | solution.py:116
  190.3 8.6 %copy.102 = bf16[4,32,48,768]{3,2,0,1:T(8,128)(2,1)} copy(bf16[4,32,48,768]{3,2,1,0:T(8,128)(2,1)} %bitcast.60) | data formatting | bytes 18874368 | tf_op jit(solution)/shard_map/reshape | solution.py:121
  198.9 5.2 %all-to-all-start.2 = ((bf16[4,32,48,768]{3,2,0,1:T(8,128)(2,1)}), bf16[4,32,48,768]{3,2,0,1:T(8,128)(2,1)}, u32[]{:S(2)}, u32[]{:S(2)}) async-start(bf16[4,32,48,768]{3,2,0,1:T(8,128)(2,1)} %copy.102), calls=%async_computation.2 | async-start | bytes 18874368 | tf_op jit(solution)/shard_map/all_to_all | solution.py:122
  204.2 0.0 reduce-scatter.2.cloned.1.call-start
  204.2 12.2 %convolution_convert_fusion = bf16[4,512,768]{2,1,0:T(8,128)(2,1)} fusion(bf16[4,1536,768]{2,1,0:T(8,128)(2,1)} %bitcast.58, f32[4,1536,512]{1,2,0:T(8,128)} %get-tuple-element.16, f32[4,1536]{1,0:T(4,128)S(1)} %sub.72, s32[4,1536]{1,0:T(4,128)S(1)} %copy-done.3, f32[4,1536]{1,0:T(4,128)S(1)} %bitcast.73), kind=kOutput, calls=%fused_computation.25 | convolution fusion | flops 4852285440 | bytes 25239552 | tf_op jit(solution)/shard_map/csl,csd->cld/dot_general | solution.py:126
  216.5 0.0 reduce-scatter.2.cloned.1.call-update
  216.5 0.6 sub.71
  217.1 120.3 %all-gather = f32[32,4,768]{2,1,0:T(4,128)S(1)} all-gather(f32[1,4,768]{2,1,0:T(4,128)S(1)} %bitcast.77), channel_id=1, replica_groups=mesh['dp'=4,'label'=32] {'label'}, dimensions={0}, use_global_device_ids=true | all-gather | bytes 405504 | tf_op jit(solution)/shard_map/all_gather | solution.py:132
  337.3 0.9 reshape.141
  338.2 2.6 convert_element_type.53
  340.8 7.3 %fusion.15 = f32[256,768]{1,0:T(8,128)} fusion(bf16[4,32,48,768]{3,2,0,1:T(8,128)(2,1)} %all-to-all-done.2, f32[4,32,256]{2,1,0:T(8,128)S(1)} %convolution_bitcast_fusion.1, pred[4,32,256]{2,1,0:T(8,128)(4,1)S(1)} %copy.88), kind=kOutput, calls=%fused_computation.30 | convolution fusion | flops 2419064832 | bytes 10387456 | tf_op jit(solution)/shard_map/cori,cord->id/dot_general | solution.py:123
  (25 shorter events, 0.2 us)
Async XLA Ops:
  7.2 94.6 %copy-start = (bf16[4,512,768]{2,1,0:T(8,128)(2,1)S(1)}, bf16[4,512,768]{2,1,0:T(8,128)(2,1)}, u32[]{:S(2)}) copy-start(bf16[4,512,768]{2,1,0:T(8,128)(2,1)} %param.6) | copy-start | bytes 9437188
  7.2 69.4 %all-gather.3.cloned.1.call-start = ((), (), s32[]{:S(2)}) async-start(), calls=%async_computation.5 | async-start | bytes 12976128 | tf_op jit(solution)/shard_map/all_gather | solution.py:74
  21.3 92.3 %copy-start.2 = (s32[4,1536]{1,0:T(4,128)}, s32[4,1536]{1,0:T(4,128)S(1)}, u32[]{:S(2)}) copy-start(s32[4,1536]{1,0:T(4,128)S(1)} %sub.68) | copy-start | bytes 73732
  124.8 12.8 %all-to-all-start = ((f32[32,1,576]{2,1,0:T(1,128)}), f32[32,1,576]{2,1,0:T(1,128)S(1)}, u32[]{:S(2)}, u32[]{:S(2)}) async-start(f32[32,1,576]{2,1,0:T(1,128)} %reshape.149), calls=%async_computation | async-start | bytes 163840 | tf_op jit(solution)/shard_map/all_to_all | solution.py:16
  160.4 17.5 %copy-start.3 = (s32[4,1536]{1,0:T(4,128)S(1)}, s32[4,1536]{1,0:T(4,128)}, u32[]{:S(2)}) copy-start(s32[4,1536]{1,0:T(4,128)} %copy-done.2) | copy-start | bytes 73732
  160.4 17.5 %copy-start.4 = (f32[4,768]{1,0:T(4,128)S(1)}, f32[4,768]{1,0:T(4,128)}, u32[]{:S(2)}) copy-start(f32[4,768]{1,0:T(4,128)} %get-tuple-element.13) | copy-start | bytes 36868
  173.8 25.1 %all-to-all-start.3 = ((f32[4,4,768]{2,1,0:T(4,128)}), f32[4,4,768]{2,1,0:T(4,128)S(1)}, u32[]{:S(2)}, u32[]{:S(2)}) async-start(f32[4,4,768]{2,1,0:T(4,128)} %broadcast_in_dim.113), calls=%async_computation.4 | async-start | bytes 98304 | tf_op jit(solution)/shard_map/all_to_all | solution.py:22
  198.9 141.9 %all-to-all-start.2 = ((bf16[4,32,48,768]{3,2,0,1:T(8,128)(2,1)}), bf16[4,32,48,768]{3,2,0,1:T(8,128)(2,1)}, u32[]{:S(2)}, u32[]{:S(2)}) async-start(bf16[4,32,48,768]{3,2,0,1:T(8,128)(2,1)} %copy.102), calls=%async_computation.2 | async-start | bytes 18874368 | tf_op jit(solution)/shard_map/all_to_all | solution.py:122
  204.2 134.0 %reduce-scatter.2.cloned.1.call-start = ((), (), s32[]{:S(2)}) async-start(), calls=%async_computation.6 | async-start | bytes 3932160 | tf_op jit(solution)/shard_map/reduce_scatter | solution.py:127
  338.2 9.8 %copy-start.1 = (bf16[4,512,768]{2,1,0:T(8,128)(2,1)S(1)}, bf16[4,512,768]{2,1,0:T(8,128)(2,1)}, u32[]{:S(2)}) copy-start(bf16[4,512,768]{2,1,0:T(8,128)(2,1)} %param.6) | copy-start | bytes 9437188
Sparse Core Ops, SparseCore 0:
  10.2 66.2 all-gather.2
  216.6 40.0 reduce-scatter.1
where the time goes:
time: 357 us; the launch traced here: 355 us
  blocking collectives  131 us (37%)
  matrix products  66 us (18%)
  waiting for transfers between devices  59.5 us (17%)
  other arithmetic  39.8 us (11%)
  local copies, waits for them, and re-layouts  29.2 us (8%)
  starting transfers between devices  14.9 us (4%)
  between operations  14.3 us (4%)
    all_gather x1, blocking collectives, body(): matcher_grads = lax.all_gather(local_sum, 'label', axis=0, tiled=True)  120 us
    all_gather x1, waiting for transfers between devices, body(): lax.all_gather(queries, 'label', axis=0, tiled=True)  53.8 us
    dot_general x1, matrix products, body(): jnp.einsum('csl,cld->csd', delta_b, labels, preferred_element_type=jnp.fl...  12.4 us
    dot_general x1, matrix products, body(): jnp.einsum('csl,csd->cld', delta_b, received, preferred_element_type=jnp....  12.2 us
    dot_general x1, matrix products, body(): jnp.einsum('csd,cld->csl', received, labels, preferred_element_type=jnp.f...  11.7 us
    dot_general x1, matrix products, body(): jnp.einsum('csri,sid->csrd', select_recv.astype(jnp.bfloat16), group, pre...  10.8 us
    all_to_all x1, blocking collectives, body(): lax.all_to_all(outgoing_lse, 'label', split_axis=1, concat_axis=1, tiled=...  10.8 us
    reshape x1, local copies, waits for them, and re-layouts, body(): slot_grad.astype(jnp.bfloat16).reshape(cl_dev, n_label, capacity, width)  8.6 us
  transfers between devices with their start and end apart: 5, of which 2 were waited for; matrix products, arithmetic and copies ran while one was open for 15% of the time, Pallas kernels for 0%

commit v1 on v0

--- a/solution.py
+++ b/solution.py
@@ -54,7 +54,6 @@
     rank_own = earlier_counts(named_own[None])[0]
     select_own = named_own.T[:, None, :] & (rank_own.T[:, None, :] == slot_iota[None, :, None])
     select_own = select_own.reshape(n_label, cl_dev, capacity, q_dev).transpose(1, 0, 2, 3)
-    select_num = select_own.astype(jnp.bfloat16)
     group_ids = cluster_ids.reshape(n_label, q_dev, K) - first
     group_pos = positives.reshape(n_label, q_dev)
     local_iota = jnp.arange(cl_dev, dtype=jnp.int32)
@@ -119,10 +118,18 @@
         + coef_b.astype(jnp.float32)[:, :, None] * match_own.astype(jnp.float32)[:, None, :]
     )
     slot_grad = slot_grad.astype(jnp.bfloat16).reshape(cl_dev, n_label, capacity, width)
-    returned = lax.all_to_all(slot_grad, "label", split_axis=1, concat_axis=1, tiled=True)
-    query_grads = jnp.einsum(
-        "cori,cord->id", select_num, returned, preferred_element_type=jnp.float32
+    partial = jnp.einsum(
+        "csri,csrd->sid",
+        select_recv.astype(jnp.bfloat16),
+        slot_grad,
+        preferred_element_type=jnp.float32,
     )
+    query_grads = lax.psum_scatter(
+        partial.astype(jnp.bfloat16).reshape(n_label * q_dev, width),
+        "label",
+        scatter_dimension=0,
+        tiled=True,
+    ).astype(jnp.float32)
     label_part = jnp.einsum("csl,csd->cld", delta_b, received, preferred_element_type=jnp.float32)
     label_grads = lax.psum_scatter(
         label_part.astype(jnp.bfloat16), "dp", scatter_dimension=1, tiled=True

time: 357 us -> 332 us (0.930)
  blocking collectives: 131 us -> 36.1 us
  waiting for transfers between devices: 59.5 us -> 133 us
  starting transfers between devices: 14.9 us -> 9.75 us
  local copies, waits for them, and re-layouts: 29.2 us -> 24.2 us
  matrix products: 66 us -> 69.8 us
    all_gather x1, blocking collectives: 120 us -> 25.2 us  [body(): matcher_grads = lax.all_gather(local_sum, 'label', axis=0, tiled=True)]
    reduce_scatter x0 -> x1, waiting for transfers between devices: none -> 69.1 us  [body(): lax.psum_scatter(partial.astype(jnp.bfloat16).reshape(n_label * q_dev, wi...]
    reshape x1 -> x0, local copies, waits for them, and re-layouts: 8.6 us -> none  [body(): slot_grad.astype(jnp.bfloat16).reshape(cl_dev, n_label, capacity, width)]
    all_to_all x1 -> x0, starting transfers between devices: 5.24 us -> none  [body(): lax.all_to_all(slot_grad, 'label', split_axis=1, concat_axis=1, tiled=True)]
    all_to_all x1, waiting for transfers between devices: 0.01 us -> 3.82 us  [sent_to_all(): lax.all_to_all(jnp.broadcast_to(shard[None], (devices, *shard.shape)), ax...]
  transfers between devices with their start and end apart: 5 -> 5, of which waited for: 2 -> 4; matrix products, arithmetic and copies ran while one was open for 15% -> 17% of each run, Pallas kernels for 0% -> 0%
where the time goes in v1:
time: 332 us; the launch traced here: 329 us
  waiting for transfers between devices  133 us (40%)
  matrix products  69.8 us (21%)
  other arithmetic  43 us (13%)
  blocking collectives  36.1 us (11%)
  local copies, waits for them, and re-layouts  24.2 us (7%)
  between operations  14 us (4%)
  starting transfers between devices  9.75 us (3%)
    reduce_scatter x1, waiting for transfers between devices, body(): lax.psum_scatter(partial.astype(jnp.bfloat16).reshape(n_label * q_dev, wi...  69.1 us
    all_gather x1, waiting for transfers between devices, body(): lax.all_gather(queries, 'label', axis=0, tiled=True)  54.5 us
    all_gather x1, blocking collectives, body(): matcher_grads = lax.all_gather(local_sum, 'label', axis=0, tiled=True)  25.2 us
    dot_general x1, matrix products, body(): jnp.einsum('csl,cld->csd', delta_b, labels, preferred_element_type=jnp.fl...  12.5 us
    dot_general x1, matrix products, body(): jnp.einsum('csd,cld->csl', received, labels, preferred_element_type=jnp.f...  12.3 us
    dot_general x1, matrix products, body(): jnp.einsum('csl,csd->cld', delta_b, received, preferred_element_type=jnp....  12.2 us
    dot_general x1, matrix products, body(): jnp.einsum('csri,sid->csrd', select_recv.astype(jnp.bfloat16), group, pre...  10.8 us
    all_to_all x1, blocking collectives, body(): lax.all_to_all(outgoing_lse, 'label', split_axis=1, concat_axis=1, tiled=...  10.8 us
  transfers between devices with their start and end apart: 5, of which 4 were waited for; matrix products, arithmetic and copies ran while one was open for 17% of the time, Pallas kernels for 0%

profile of v1, /device:TPU:1, one launch (start us, length us, event | category | flops | bytes accessed | tf_op | source)
XLA Modules:
  0.0 329.4 jit_solution(1523376912669053835)
XLA Ops:
  7.2 0.0 all-gather.3.cloned.1.call-start
  7.2 0.7 all-gather.3.cloned.1.call-update
  7.9 1.0 reshape.140
  8.9 0.7 constant_dynamic-slice_fusion
  9.6 0.1 copy.68
  9.7 1.6 fusion.15
  11.3 0.1 copy.69
  11.5 0.8 add_select_fusion.1
  12.3 1.9 select_reduce_fusion.6
  14.2 0.6 eq.121
  14.8 1.1 copy.111
  15.9 0.5 fusion.16
  16.4 0.2 convolution_bitcast_fusion
  16.6 0.1 copy.74
  16.7 0.8 select_add_fusion
  17.5 2.3 select_reduce_fusion.5
  19.8 0.7 sub.68
  20.5 1.3 dynamic-slice_convert_fusion
  21.8 0.2 convolution_bitcast_fusion.1
  22.0 54.5 %all-gather.3.cloned.1.call-done = bf16[8192,768]{1,0:T(8,128)(2,1)} async-done(((bf16[256,768]{1,0:T(8,128)(2,1)}), bf16[8192,768]{1,0:T(8,128)(2,1)}) %all-gather.3.cloned.1.call-update) | async-done | bytes 12582928 | tf_op jit(solution)/shard_map/all_gather | solution.py:73
  76.6 10.8 %convert_bitcast_fusion = bf16[4,32,48,768]{3,2,0,1:T(8,128)(2,1)} fusion(bf16[32,256,768,1]{2,1,3,0:T(8,128)(2,1)} %bitcast.59, f32[4,32,256]{2,0,1:T(4,128)S(1)} %copy.74, pred[4,32,256]{2,0,1:T(4,128)(4,1)S(1)} %bitcast.66), kind=kOutput, calls=%fused_computation.9 | convolution fusion | flops 2423783424 | bytes 22183936 | tf_op jit(solution)/shard_map/csri,sid->csrd/dot_general | solution.py:74
  87.4 8.1 %copy.75 = bf16[4,32,48,768]{3,2,1,0:T(8,128)(2,1)} copy(bf16[4,32,48,768]{3,2,0,1:T(8,128)(2,1)} %convert_bitcast_fusion) | data formatting | bytes 18874368 | tf_op jit(solution)/shard_map/convert_element_type | solution.py:80
  95.5 6.2 %fusion.27 = f32[4,1,1536]{2,1,0:T(1,128)S(1)} fusion(bf16[4,1536,768]{2,1,0:T(8,128)(2,1)} %bitcast.55, bf16[4,768,1]{1,0,2:T(4,128)(2,1)S(1)} %get-tuple-element.14), kind=kOutput, calls=%fused_computation.61 | convolution fusion | flops 9437184 | bytes 9467904 | tf_op jit(solution)/shard_map/csd,cd->cs/dot_general | solution.py:83
  101.8 12.3 %add_reduce_fusion = (f32[4,1536]{1,0:T(4,128)}, f32[4,1536,512]{1,2,0:T(8,128)}) fusion(f32[4,1536]{1,0:T(4,128)S(1)} %bitcast.70, bf16[4,1536,768]{2,1,0:T(8,128)(2,1)} %bitcast.56, bf16[4,512,768]{2,1,0:T(8,128)(2,1)S(1)} %copy-done), kind=kOutput, calls=%fused_computation.6 | convolution fusion | flops 4838123520 | bytes 25214976 | tf_op jit(solution)/shard_map/csd,cld->csl/dot_general | solution.py:82
  114.1 0.8 reshape.138
  115.0 7.7 %exponential_reduce_fusion = (f32[4,1536]{1,0:T(4,128)}, f32[4,1536]{1,0:T(4,128)}) fusion(f32[4,1536,512]{1,2,0:T(8,128)} %get-tuple-element.16, f32[4,1536]{1,0:T(4,128)} %get-tuple-element.15, f32[4,1536]{1,0:T(4,128)} %bitcast.71, s32[4,1536]{1,0:T(4,128)} %sub.68), kind=kLoop, calls=%fused_computation.5 | loop fusion | flops 18862080 | bytes 12705792 | tf_op jit(solution)/shard_map/reduce_sum | solution.py:90
  122.6 1.5 reshape.139
  124.1 1.5 reshape.141
  125.6 0.9 pad_maximum_fusion
  126.4 0.8 copy.114
  127.3 1.8 reshape.153
  129.0 5.4 %all-to-all-start = ((f32[32,1,576]{2,1,0:T(1,128)}), f32[32,1,576]{2,1,0:T(1,128)S(1)}, u32[]{:S(2)}, u32[]{:S(2)}) async-start(f32[32,1,576]{2,1,0:T(1,128)} %reshape.153), calls=%async_computation | async-start | bytes 163840 | tf_op jit(solution)/shard_map/all_to_all | solution.py:16
  134.5 0.0 reduce-scatter.5.cloned.1.call-start
  134.5 2.9 fusion.7
  137.4 4.4 %all-to-all-done = f32[32,1,576]{2,1,0:T(1,128)S(1)} async-done(((f32[32,1,576]{2,1,0:T(1,128)}), f32[32,1,576]{2,1,0:T(1,128)S(1)}, u32[]{:S(2)}, u32[]{:S(2)}) %all-to-all-start) | async-done | bytes 73760 | tf_op jit(solution)/shard_map/all_to_all | solution.py:16
  141.8 0.5 broadcast.125
  142.3 1.5 reduce.1
  143.8 1.7 reshape.154
  145.5 1.1 fusion.31
  146.6 1.7 select_reduce_fusion.4
  148.4 2.4 select_reduce_fusion.3
  150.8 3.4 %select_reduce_fusion.1 = (f32[4,32,48]{2,1,0:T(8,128)S(1)}, f32[256]{0:T(256)S(1)}) fusion(f32[256]{0:T(256)S(1)} %log_add_fusion, f32[4,32,256]{2,1,0:T(8,128)S(1)} %convolution_bitcast_fusion.1, pred[4,32,256]{2,1,0:T(8,128)(4,1)S(1)} %copy.70, f32[4,32,48]{2,1,0:T(8,128)S(1)} %copy.80), kind=kLoop, calls=%fused_computation.12 | loop fusion | flops 9430784 | bytes 215040 | tf_op jit(solution)/shard_map/reduce_sum | solution.py:106
  154.2 0.7 broadcast_select_fusion
  155.0 0.1 reshape.155
  155.1 10.8 %all_to_all.15 = f32[32,1,192]{2,1,0:T(1,128)S(1)} all-to-all(f32[32,1,192]{2,1,0:T(1,128)S(1)} %reshape.155), channel_id=1, replica_groups=mesh['dp'=4,'label'=32] {'label'}, dimensions={0} | all-to-all | bytes 49152 | tf_op jit(solution)/shard_map/all_to_all | solution.py:108
  166.0 0.7 reduce.2
  166.7 0.1 reshape.156
  166.8 0.1 sub.72
  166.9 12.2 %convolution_convert_fusion = bf16[4,512,768]{2,1,0:T(8,128)(2,1)} fusion(bf16[4,1536,768]{2,1,0:T(8,128)(2,1)} %bitcast.57, f32[4,1536,512]{1,2,0:T(8,128)} %get-tuple-element.16, f32[4,1536]{1,0:T(4,128)S(1)} %sub.72, s32[4,1536]{1,0:T(4,128)} %sub.68, f32[4,1536]{1,0:T(4,128)} %bitcast.72), kind=kOutput, calls=%fused_computation.26 | convolution fusion | flops 4852285440 | bytes 25239552 | tf_op jit(solution)/shard_map/csl,csd->cld/dot_general | solution.py:133
  179.2 0.0 reduce-scatter.3.cloned.1.call-start
  179.2 7.0 %fusion.2 = bf16[4,1536]{1,0:T(4,128)(2,1)S(1)} fusion(f32[4,1536,512]{1,2,0:T(8,128)} %get-tuple-element.16, f32[4,1536]{1,0:T(4,128)S(1)} %sub.72, s32[4,1536]{1,0:T(4,128)S(1)} %copy-done.3, f32[4,1536]{1,0:T(4,128)S(1)} %bitcast.73), kind=kLoop, calls=%fused_computation.10 | loop fusion | flops 18868224 | bytes 12668928 | tf_op jit(solution)/shard_map/reduce_sum | solution.py:112
  186.3 12.5 %add_convert_fusion = bf16[4,1536,768]{2,1,0:T(8,128)(2,1)} fusion(f32[4,768]{1,0:T(4,128)S(1)} %copy-done.4, f32[4,1536]{1,0:T(4,128)S(1)} %convert_element_type.80, bf16[4,512,768]{2,1,0:T(8,128)(2,1)S(1)} %copy-done, f32[4,1536,512]{1,2,0:T(8,128)} %get-tuple-element.16, f32[4,1536]{1,0:T(4,128)S(1)} %sub.72, s32[4,1536]{1,0:T(4,128)S(1)} %copy-done.3, ...), kind=kOutput, calls=%fused_computation.1 | convolution fusion | flops 4864868352 | bytes 25276416 | tf_op jit(solution)/shard_map/csl,cld->csd/dot_general | solution.py:115
  198.8 10.2 %bitcast_convert_fusion = bf16[32,256,768]{2,1,0:T(8,128)(2,1)} fusion(bf16[4,32,48,768]{3,2,1,0:T(8,128)(2,1)} %bitcast.80, f32[4,32,256]{2,0,1:T(4,128)S(1)} %copy.74, pred[4,32,256]{2,0,1:T(4,128)(4,1)S(1)} %bitcast.67), kind=kOutput, calls=%fused_computation | convolution fusion | flops 2425356288 | bytes 22183936 | tf_op jit(solution)/shard_map/csri,csrd->sid/dot_general | solution.py:121
  208.9 0.0 reduce-scatter.3.cloned.1.call-update
  209.0 5.1 %fusion.25 = f32[4,1,768]{2,1,0:T(1,128)S(1)} fusion(bf16[4,1536,768]{2,1,0:T(8,128)(2,1)} %bitcast.58, bf16[4,1536,1]{1,0,2:T(4,128)(2,1)S(1)} %bitcast.75), kind=kOutput, calls=%fused_computation.57 | convolution fusion | flops 9437184 | bytes 9461760 | tf_op jit(solution)/shard_map/cs,csd->cd/dot_general | solution.py:137
  214.0 0.6 broadcast_in_dim.113
  214.7 4.2 %all-to-all-start.2 = ((f32[4,4,768]{2,1,0:T(4,128)}), f32[4,4,768]{2,1,0:T(4,128)S(1)}, u32[]{:S(2)}, u32[]{:S(2)}) async-start(f32[4,4,768]{2,1,0:T(4,128)} %broadcast_in_dim.113), calls=%async_computation.4 | async-start | bytes 98304 | tf_op jit(solution)/shard_map/all_to_all | solution.py:22
  218.9 0.6 sub.71
  219.4 3.8 %all-to-all-done.2 = f32[4,4,768]{2,1,0:T(4,128)S(1)} async-done(((f32[4,4,768]{2,1,0:T(4,128)}), f32[4,4,768]{2,1,0:T(4,128)S(1)}, u32[]{:S(2)}, u32[]{:S(2)}) %all-to-all-start.2) | async-done | bytes 49184 | tf_op jit(solution)/shard_map/all_to_all | solution.py:22
  223.3 25.2 %all-gather = f32[32,4,768]{2,1,0:T(4,128)S(1)} all-gather(f32[1,4,768]{2,1,0:T(4,128)S(1)} %bitcast.78), channel_id=1, replica_groups=mesh['dp'=4,'label'=32] {'label'}, dimensions={0}, use_global_device_ids=true | all-gather | bytes 405504 | tf_op jit(solution)/shard_map/all_gather | solution.py:139
  248.5 0.9 reshape.145
  249.4 2.4 convert_element_type.61
  251.9 69.1 %reduce-scatter.3.cloned.1.call-done = bf16[256,768]{1,0:T(8,128)(2,1)} async-done(((bf16[8192,768]{1,0:T(8,128)(2,1)}), bf16[256,768]{1,0:T(8,128)(2,1)}) %reduce-scatter.3.cloned.1.call-update) | async-done | bytes 393232 | tf_op jit(solution)/shard_map/reduce_scatter | solution.py:127
  321.0 1.9 convert_element_type.59
  (26 shorter events, 0.2 us)
Async XLA Ops:
  7.2 94.6 %copy-start = (bf16[4,512,768]{2,1,0:T(8,128)(2,1)S(1)}, bf16[4,512,768]{2,1,0:T(8,128)(2,1)}, u32[]{:S(2)}) copy-start(bf16[4,512,768]{2,1,0:T(8,128)(2,1)} %param.6) | copy-start | bytes 9437188
  7.2 69.4 %all-gather.3.cloned.1.call-start = ((), (), s32[]{:S(2)}) async-start(), calls=%async_computation.5 | async-start | bytes 12976128 | tf_op jit(solution)/shard_map/all_gather | solution.py:73
  101.8 12.4 %copy-start.1 = (f32[4,1,1536]{2,0,1:T(4,128)}, f32[4,1,1536]{2,0,1:T(4,128)S(1)}, u32[]{:S(2)}) copy-start(f32[4,1,1536]{2,0,1:T(4,128)S(1)} %copy.112) | copy-start | bytes 73732
  129.0 12.8 %all-to-all-start = ((f32[32,1,576]{2,1,0:T(1,128)}), f32[32,1,576]{2,1,0:T(1,128)S(1)}, u32[]{:S(2)}, u32[]{:S(2)}) async-start(f32[32,1,576]{2,1,0:T(1,128)} %reshape.153), calls=%async_computation | async-start | bytes 163840 | tf_op jit(solution)/shard_map/all_to_all | solution.py:16
  134.5 114.9 %reduce-scatter.5.cloned.1.call-start = ((), (), s32[]{:S(2)}) async-start(), calls=%async_computation.7 | async-start | bytes 3932160 | tf_op jit(solution)/shard_map/reduce_scatter | solution.py:134
  166.9 12.3 %copy-start.2 = (f32[4,1,1536]{2,0,1:T(4,128)S(1)}, f32[4,1,1536]{2,0,1:T(4,128)}, u32[]{:S(2)}) copy-start(f32[4,1,1536]{2,0,1:T(4,128)} %copy-done.1) | copy-start | bytes 73732
  166.9 12.3 %copy-start.3 = (s32[4,1536]{1,0:T(4,128)S(1)}, s32[4,1536]{1,0:T(4,128)}, u32[]{:S(2)}) copy-start(s32[4,1536]{1,0:T(4,128)} %sub.68) | copy-start | bytes 73732
  179.1 7.1 %copy-start.4 = (f32[4,768]{1,0:T(4,128)S(1)}, f32[4,768]{1,0:T(4,128)}, u32[]{:S(2)}) copy-start(f32[4,768]{1,0:T(4,128)} %get-tuple-element.13) | copy-start | bytes 36868
  179.2 141.8 %reduce-scatter.3.cloned.1.call-start = ((), (), s32[]{:S(2)}) async-start(), calls=%async_computation.6 | async-start | bytes 12976128 | tf_op jit(solution)/shard_map/reduce_scatter | solution.py:127
  214.7 8.6 %all-to-all-start.2 = ((f32[4,4,768]{2,1,0:T(4,128)}), f32[4,4,768]{2,1,0:T(4,128)S(1)}, u32[]{:S(2)}, u32[]{:S(2)}) async-start(f32[4,4,768]{2,1,0:T(4,128)} %broadcast_in_dim.113), calls=%async_computation.4 | async-start | bytes 98304 | tf_op jit(solution)/shard_map/all_to_all | solution.py:22
Sparse Core Ops, SparseCore 0:
  10.2 66.2 all-gather.2
  179.3 35.8 reduce-scatter.4
  219.0 101.8 reduce-scatter.2

commit v2 on v1

--- a/solution.py
+++ b/solution.py
@@ -1,6 +1,8 @@
 import jax
 import jax.numpy as jnp
 from jax import lax
+from jax.experimental import pallas as pl
+from jax.experimental.pallas import tpu as pltpu
 from jax.sharding import PartitionSpec as P
 
 LEAF = 512
@@ -35,6 +37,190 @@
     return jnp.einsum(
         "ij,sjc->sic", lower, named.astype(jnp.bfloat16), preferred_element_type=jnp.float32
     )
+
+
+MESH = pl.DeviceIdType.MESH
+
+def place():
+    me = lax.axis_index("label")
+    core = lax.rem(me, 2)
+    x = lax.rem(me // 2, 4)
+    y = me // 8
+    a = x * (1 - core) + y * core
+    b = y * (1 - core) + x * core
+    return me, core, a, b
+
+def index_of(core, a, b):
+    x = a * (1 - core) + b * core
+    y = b * (1 - core) + a * core
+    return (y * 4 + x) * 2 + core
+
+OFF = (0, 3, 1, 2)
+
+class Links:
+    def __init__(self, send, recv):
+        self.me, self.core, self.a, self.b = place()
+        self.send, self.recv, self.sent = send, recv, []
+        c, a, b = self.core, self.a, self.b
+        self.partner = self.me + 1 - 2 * c
+        self.dev = {
+            "a-": index_of(c, lax.rem(a + 3, 4), b),
+            "a+": index_of(c, lax.rem(a + 1, 4), b),
+            "b-": index_of(c, a, lax.rem(b + 3, 4)),
+            "b+": index_of(c, a, lax.rem(b + 1, 4)),
+            "p": self.partner,
+        }
+    def block(self, i, j):
+        return index_of(self.core, lax.rem(self.a + OFF[i], 4), lax.rem(self.b + OFF[j], 4))
+    def partner_block(self, i, j):
+        return index_of(1 - self.core, lax.rem(self.b + OFF[i], 4), lax.rem(self.a + OFF[j], 4))
+    def meet(self):
+        barrier = pltpu.get_barrier_semaphore()
+        for d in self.dev.values():
+            pl.semaphore_signal(barrier, inc=1, device_id={"label": d}, device_id_type=MESH)
+        pl.semaphore_wait(barrier, 5)
+    def copy(self, src, dst, slot, to):
+        n = len(self.sent)
+        c = pltpu.make_async_remote_copy(src_ref=src, dst_ref=dst, send_sem=self.send.at[n],
+            recv_sem=self.recv.at[slot], device_id={"label": self.dev[to]}, device_id_type=MESH)
+        c.start()
+        self.sent.append(c)
+    def wait(self, dst, slot):
+        pltpu.make_async_remote_copy(src_ref=dst, dst_ref=dst, send_sem=self.send.at[0],
+            recv_sem=self.recv.at[slot], device_id={"label": self.partner}, device_id_type=MESH).wait_recv()
+    def drain(self):
+        for c in self.sent:
+            c.wait_send()
+
+def gather_kernel(q_ref, g, send, recv):
+    L = Links(send, recv)
+    L.meet()
+    half = q_ref.shape[0] // 2
+    lo = lambda k: g.at[k, pl.ds(0, half)]
+    hi = lambda k: g.at[k, pl.ds(half, half)]
+    own = L.block(0, 0)
+    for to, slot in (("a+", 0), ("a-", 1), ("b+", 4), ("b-", 5), ("p", 20)):
+        L.copy(q_ref, g.at[own], slot, to)
+    g[own] = q_ref[...]
+    def side_a(i):
+        k = L.block(i, 0)
+        L.wait(g.at[k], i - 1)
+        if i == 1:
+            L.copy(lo(k), lo(k), 2, "a+")
+        else:
+            L.copy(hi(k), hi(k), 3, "a-")
+        L.copy(g.at[k], g.at[k], 4 + 4 * i, "b+")
+        L.copy(g.at[k], g.at[k], 5 + 4 * i, "b-")
+        L.copy(g.at[k], g.at[k], 20 + 4 * i, "p")
+    def far_a():
+        k = L.block(3, 0)
+        L.wait(lo(k), 2)
+        L.wait(hi(k), 3)
+        L.copy(g.at[k], g.at[k], 16, "b+")
+        L.copy(g.at[k], g.at[k], 17, "b-")
+        L.copy(g.at[k], g.at[k], 32, "p")
+    def side_b(i):
+        k = L.block(i, 1)
+        L.wait(g.at[k], 4 + 4 * i)
+        L.copy(lo(k), lo(k), 6 + 4 * i, "b+")
+        L.copy(g.at[k], g.at[k], 21 + 4 * i, "p")
+        k = L.block(i, 2)
+        L.wait(g.at[k], 5 + 4 * i)
+        L.copy(hi(k), hi(k), 7 + 4 * i, "b-")
+        L.copy(g.at[k], g.at[k], 22 + 4 * i, "p")
+    def far_b(i):
+        k = L.block(i, 3)
+        L.wait(lo(k), 6 + 4 * i)
+        L.wait(hi(k), 7 + 4 * i)
+        L.copy(g.at[k], g.at[k], 23 + 4 * i, "p")
+    def from_partner(i, j):
+        k = L.partner_block(i, j)
+        L.wait(g.at[k], 20 + 4 * i + j)
+    side_a(1); side_a(2); side_b(0); far_a(); side_b(1); far_b(0); side_b(2); far_b(1); side_b(3); far_b(2); far_b(3)
+    for i in range(4):
+        for j in range(4):
+            from_partner(i, j)
+    L.drain()
+
+def gather(q):
+    return pl.pallas_call(
+        gather_kernel,
+        out_shape=jax.ShapeDtypeStruct((32, *q.shape), q.dtype),
+        in_specs=[pl.BlockSpec(memory_space=pltpu.VMEM)],
+        out_specs=pl.BlockSpec(memory_space=pltpu.VMEM),
+        scratch_shapes=[pltpu.SemaphoreType.DMA((36,)), pltpu.SemaphoreType.DMA((36,))],
+        compiler_params=pltpu.CompilerParams(collective_id=0, has_side_effects=True),
+    )(q)
+
+def scatter_kernel(p, out, t, u, pr, bh, bf, ah, af, send, recv):
+    L = Links(send, recv)
+    L.meet()
+    half = p.shape[1] // 2
+    f32 = jnp.float32
+    ORDER = [(i, 3) for i in (3, 1, 2, 0)] + [(i, j) for i in (3, 1, 2, 0) for j in (1, 2)] + [(i, 0) for i in (3, 1, 2, 0)]
+    for i, j in ORDER:
+        L.copy(p.at[L.partner_block(i, j)], pr.at[4 * i + j], 4 * i + j, "p")
+    LO, HI = pl.ds(0, half), pl.ds(half, half)
+    def both(i, j):
+        L.wait(pr.at[4 * i + j], 4 * i + j)
+        return lambda s: p[L.block(i, j), s].astype(f32) + pr[4 * i + j, s].astype(f32)
+    for i in (3, 1, 2, 0):
+        s = both(i, 3)
+        n = 3 * i + 2
+        t[n] = s(slice(None)).astype(t.dtype)
+        L.copy(t.at[n, LO], bh.at[i, 0], 16 + 4 * i, "b+")
+        L.copy(t.at[n, HI], bh.at[i, 1], 17 + 4 * i, "b-")
+    for i in (3, 1, 2, 0):
+        s = both(i, 2)
+        n = 3 * i + 1
+        L.wait(bh.at[i, 0], 16 + 4 * i)
+        t[n, LO] = (s(LO) + bh[i, 0].astype(f32)).astype(t.dtype)
+        t[n, HI] = s(HI).astype(t.dtype)
+        L.copy(t.at[n], bf.at[i, 0], 18 + 4 * i, "b+")
+        s = both(i, 1)
+        n = 3 * i
+        L.wait(bh.at[i, 1], 17 + 4 * i)
+        t[n, HI] = (s(HI) + bh[i, 1].astype(f32)).astype(t.dtype)
+        t[n, LO] = s(LO).astype(t.dtype)
+        L.copy(t.at[n], bf.at[i, 1], 19 + 4 * i, "b-")
+    def column(i):
+        s = both(i, 0)
+        L.wait(bf.at[i, 0], 18 + 4 * i)
+        L.wait(bf.at[i, 1], 19 + 4 * i)
+        return lambda r: s(r) + bf[i, 0, r].astype(f32) + bf[i, 1, r].astype(f32)
+    s = column(3)
+    u[2] = s(slice(None)).astype(u.dtype)
+    L.copy(u.at[2, LO], ah.at[0], 32, "a+")
+    L.copy(u.at[2, HI], ah.at[1], 33, "a-")
+    s = column(1)
+    L.wait(ah.at[1], 33)
+    u[0, HI] = (s(HI) + ah[1].astype(f32)).astype(u.dtype)
+    u[0, LO] = s(LO).astype(u.dtype)
+    L.copy(u.at[0], af.at[1], 35, "a-")
+    s = column(2)
+    L.wait(ah.at[0], 32)
+    u[1, LO] = (s(LO) + ah[0].astype(f32)).astype(u.dtype)
+    u[1, HI] = s(HI).astype(u.dtype)
+    L.copy(u.at[1], af.at[0], 34, "a+")
+    s = column(0)
+    L.wait(af.at[0], 34)
+    L.wait(af.at[1], 35)
+    out[...] = s(slice(None)) + af[0].astype(f32) + af[1].astype(f32)
+    L.drain()
+
+def scatter(p):
+    n, r, w = p.shape
+    bf16 = jnp.bfloat16
+    return pl.pallas_call(
+        scatter_kernel,
+        out_shape=jax.ShapeDtypeStruct((r, w), jnp.float32),
+        in_specs=[pl.BlockSpec(memory_space=pltpu.VMEM)],
+        out_specs=pl.BlockSpec(memory_space=pltpu.VMEM),
+        scratch_shapes=[pltpu.VMEM((12, r, w), bf16), pltpu.VMEM((3, r, w), bf16), pltpu.VMEM((16, r, w), bf16),
+            pltpu.VMEM((4, 2, r // 2, w), bf16), pltpu.VMEM((4, 2, r, w), bf16), pltpu.VMEM((2, r // 2, w), bf16), pltpu.VMEM((2, r, w), bf16),
+            pltpu.SemaphoreType.DMA((36,)), pltpu.SemaphoreType.DMA((36,))],
+        compiler_params=pltpu.CompilerParams(collective_id=1, has_side_effects=True),
+    )(p)
 
 
 def body(queries, labels, matcher, cluster_ids, positives):
@@ -70,7 +256,7 @@
         pos_cluster[None, :, :] == local_iota[:, None, None], (group_pos % LEAF)[None, :, :], -1
     )
     target_map = jnp.sum(jnp.where(select_recv, target_val[:, :, None, :] + 1, 0), axis=3) - 1
-    group = lax.all_gather(queries, "label", axis=0, tiled=True).reshape(n_label, q_dev, width)
+    group = gather(queries)
     picked_rows = jnp.einsum(
         "csri,sid->csrd",
         select_recv.astype(jnp.bfloat16),
@@ -124,12 +310,7 @@
         slot_grad,
         preferred_element_type=jnp.float32,
     )
-    query_grads = lax.psum_scatter(
-        partial.astype(jnp.bfloat16).reshape(n_label * q_dev, width),
-        "label",
-        scatter_dimension=0,
-        tiled=True,
-    ).astype(jnp.float32)
+    query_grads = scatter(partial.astype(jnp.bfloat16))
     label_part = jnp.einsum("csl,csd->cld", delta_b, received, preferred_element_type=jnp.float32)
     label_grads = lax.psum_scatter(
         label_part.astype(jnp.bfloat16), "dp", scatter_dimension=1, tiled=True

time: 332 us -> 283 us (0.85)
  waiting for transfers between devices: 133 us -> 2.26 us
  Pallas kernels: 0 us -> 93.2 us
  other arithmetic: 43 us -> 37.1 us
  local copies, waits for them, and re-layouts: 24.2 us -> 19.9 us
    pallas_call x0 -> x2, Pallas kernels: none -> 93.2 us  [the longest x1 49.3 us: gather(): pl.pallas_call(gather_kernel, out_shape=jax.ShapeDtypeStruct((32, *q.shap...]
    reduce_scatter x1 -> x0, waiting for transfers between devices: 69.1 us -> none  [body(): lax.psum_scatter(partial.astype(jnp.bfloat16).reshape(n_label * q_dev, wi...]
    all_gather x1 -> x0, waiting for transfers between devices: 54.5 us -> none  [body(): lax.all_gather(queries, 'label', axis=0, tiled=True)]
    all_to_all x1, waiting for transfers between devices: 3.82 us -> 0.01 us  [sent_to_all(): lax.all_to_all(jnp.broadcast_to(shard[None], (devices, *shard.shape)), ax...]
  transfers between devices with their start and end apart: 5 -> 3, of which waited for: 4 -> 1; matrix products, arithmetic and copies ran while one was open for 17% -> 15% of each run, Pallas kernels for 0% -> 16%
where the time goes in v2:
time: 283 us; the launch traced here: 282 us
  Pallas kernels  93.2 us (33%)
  matrix products  69.3 us (24%)
  other arithmetic  37.1 us (13%)
  blocking collectives  36.7 us (13%)
  local copies, waits for them, and re-layouts  19.9 us (7%)
  between operations  14.4 us (5%)
  starting transfers between devices  9.02 us (3%)
    pallas_call x1, Pallas kernels, gather(): pl.pallas_call(gather_kernel, out_shape=jax.ShapeDtypeStruct((32, *q.shap...  49.3 us
    pallas_call x1, Pallas kernels, scatter(): pl.pallas_call(scatter_kernel, out_shape=jax.ShapeDtypeStruct((r, w), jnp...  44 us
    all_gather x1, blocking collectives, body(): matcher_grads = lax.all_gather(local_sum, 'label', axis=0, tiled=True)  24.5 us
    dot_general x1, matrix products, body(): jnp.einsum('csl,cld->csd', delta_b, labels, preferred_element_type=jnp.fl...  12.5 us
    dot_general x1, matrix products, body(): jnp.einsum('csl,csd->cld', delta_b, received, preferred_element_type=jnp....  12.3 us
    all_to_all x1, blocking collectives, body(): lax.all_to_all(outgoing_lse, 'label', split_axis=1, concat_axis=1, tiled=...  12.2 us
    dot_general x1, matrix products, body(): jnp.einsum('csd,cld->csl', received, labels, preferred_element_type=jnp.f...  11.7 us
    dot_general x1, matrix products, body(): jnp.einsum('csri,sid->csrd', select_recv.astype(jnp.bfloat16), group, pre...  10.8 us
  transfers between devices with their start and end apart: 3, of which 1 were waited for; matrix products, arithmetic and copies ran while one was open for 15% of the time, Pallas kernels for 16%

profile of v2, /device:TPU:1, one launch (start us, length us, event | category | flops | bytes accessed | tf_op | source)
XLA Modules:
  0.0 281.8 jit_solution(3119462871008128386)
XLA Ops:
  7.2 0.0 copy-start
  7.2 0.9 reshape.133
  8.1 0.8 add_select_fusion.1
  8.9 1.9 select_reduce_fusion.6
  10.9 1.1 copy.111
  12.0 0.5 fusion.20
  12.4 0.0 copy-start.1
  12.5 0.2 convolution_bitcast_fusion
  12.7 0.1 copy.74
  12.8 2.3 select_reduce_fusion.5
  15.1 0.1 sub.68
  15.2 0.0 copy-start.5
  15.2 49.3 %shard_map.84 = bf16[32,256,768]{2,1,0:T(8,128)(2,1)} custom-call(bf16[256,768]{1,0:T(8,128)(2,1)} %q_ref.1), custom_call_target="tpu_custom_call" | custom-call | tf_op jit(solution)/shard_map/pallas_call | solution.py:146
  64.5 10.8 %convert_bitcast_fusion = bf16[4,32,48,768]{3,2,0,1:T(8,128)(2,1)} fusion(bf16[32,256,768]{2,1,0:T(8,128)(2,1)} %shard_map.84, f32[4,32,256]{2,0,1:T(4,128)S(1)} %copy.74, pred[4,32,256]{2,0,1:T(4,128)(4,1)S(1)} %bitcast.64), kind=kOutput, calls=%fused_computation.11 | convolution fusion | flops 2423783424 | bytes 22183936 | tf_op jit(solution)/shard_map/csri,sid->csrd/dot_general | solution.py:260
  75.3 0.0 copy-done.1
  75.3 8.1 %copy.75 = bf16[4,32,48,768]{3,2,1,0:T(8,128)(2,1)} copy(bf16[4,32,48,768]{3,2,0,1:T(8,128)(2,1)} %convert_bitcast_fusion) | data formatting | bytes 18874368 | tf_op jit(solution)/shard_map/convert_element_type | solution.py:266
  83.5 1.3 dynamic-slice_convert_fusion
  84.8 6.2 %fusion.31 = f32[4,1,1536]{2,1,0:T(1,128)S(1)} fusion(bf16[4,1536,768]{2,1,0:T(8,128)(2,1)} %bitcast.55, bf16[4,768,1]{1,0,2:T(4,128)(2,1)S(1)} %get-tuple-element.14), kind=kOutput, calls=%fused_computation.63 | convolution fusion | flops 9437184 | bytes 9467904 | tf_op jit(solution)/shard_map/csd,cd->cs/dot_general | solution.py:269
  91.0 11.7 %add_reduce_fusion = (f32[4,1536]{1,0:T(4,128)S(1)}, f32[4,1536,512]{1,2,0:T(8,128)}) fusion(f32[4,1536]{1,0:T(4,128)S(1)} %bitcast.68, bf16[4,1536,768]{2,1,0:T(8,128)(2,1)} %bitcast.56, bf16[4,512,768]{2,1,0:T(8,128)(2,1)S(1)} %copy-done), kind=kOutput, calls=%fused_computation.8 | convolution fusion | flops 4838123520 | bytes 25214976 | tf_op jit(solution)/shard_map/csd,cld->csl/dot_general | solution.py:268
  102.8 0.1 reshape.131
  102.9 0.0 copy-done.5
  102.9 0.0 copy-done.3
  102.9 6.8 %exponential_reduce_fusion = (f32[4,1536]{1,0:T(4,128)S(1)}, f32[4,1536]{1,0:T(4,128)S(1)}) fusion(f32[4,1536,512]{1,2,0:T(8,128)} %get-tuple-element.16, f32[4,1536]{1,0:T(4,128)S(1)} %get-tuple-element.15, f32[4,1536]{1,0:T(4,128)S(1)} %bitcast.69, s32[4,1536]{1,0:T(4,128)S(1)} %sub.68), kind=kLoop, calls=%fused_computation.7 | loop fusion | flops 18862080 | bytes 12705792 | tf_op jit(solution)/shard_map/reduce_sum | solution.py:276
  109.7 0.1 reshape.132
  109.8 0.1 reshape.134
  109.9 0.1 copy.114
  110.1 0.8 reshape.145
  110.9 4.1 %all-to-all-start = ((f32[32,1,576]{2,1,0:T(1,128)}), f32[32,1,576]{2,1,0:T(1,128)S(1)}, u32[]{:S(2)}, u32[]{:S(2)}) async-start(f32[32,1,576]{2,1,0:T(1,128)} %reshape.145), calls=%async_computation | async-start | bytes 163840 | tf_op jit(solution)/shard_map/all_to_all | solution.py:18
  115.0 0.0 reduce-scatter.2.cloned.1.call-start
  115.0 0.7 constant_dynamic-slice_fusion
  115.8 0.1 copy.68
  115.9 1.6 fusion.19
  117.4 0.1 copy.69
  117.6 0.2 convolution_bitcast_fusion.1
  117.8 2.3 fusion.11
  120.1 2.2 all-to-all-done
  122.3 0.5 broadcast.125
  122.8 1.5 reduce.1
  124.3 1.7 reshape.146
  126.0 1.1 fusion.35
  127.1 1.7 select_reduce_fusion.4
  128.9 2.4 select_reduce_fusion.3
  131.3 3.4 %select_reduce_fusion.1 = (f32[4,32,48]{2,1,0:T(8,128)S(1)}, f32[256]{0:T(256)S(1)}) fusion(f32[256]{0:T(256)S(1)} %log_add_fusion, f32[4,32,256]{2,1,0:T(8,128)S(1)} %convolution_bitcast_fusion.1, pred[4,32,256]{2,1,0:T(8,128)(4,1)S(1)} %copy.70, f32[4,32,48]{2,1,0:T(8,128)S(1)} %copy.80), kind=kLoop, calls=%fused_computation.14 | loop fusion | flops 9430784 | bytes 215040 | tf_op jit(solution)/shard_map/reduce_sum | solution.py:292
  134.8 0.1 reshape.147
  134.9 12.2 %all_to_all.15 = f32[32,1,192]{2,1,0:T(1,128)S(1)} all-to-all(f32[32,1,192]{2,1,0:T(1,128)S(1)} %reshape.147), channel_id=1, replica_groups=mesh['dp'=4,'label'=32] {'label'}, dimensions={0} | all-to-all | bytes 49152 | tf_op jit(solution)/shard_map/all_to_all | solution.py:294
  147.1 0.7 reduce.2
  147.9 0.1 reshape.148
  148.0 0.1 sub.72
  148.1 12.3 %convolution_convert_fusion = bf16[4,512,768]{2,1,0:T(8,128)(2,1)} fusion(bf16[4,1536,768]{2,1,0:T(8,128)(2,1)} %bitcast.57, f32[4,1536,512]{1,2,0:T(8,128)} %get-tuple-element.16, f32[4,1536]{1,0:T(4,128)S(1)} %sub.72, s32[4,1536]{1,0:T(4,128)} %copy-done.5, f32[4,1536]{1,0:T(4,128)} %bitcast.70), kind=kOutput, calls=%fused_computation.28 | convolution fusion | flops 4852285440 | bytes 25239552 | tf_op jit(solution)/shard_map/csl,csd->cld/dot_general | solution.py:314
  160.4 0.0 reduce-scatter.2.cloned.1.call-update
  160.4 0.6 sub.71
  161.0 0.0 copy-done.6
  161.0 6.8 %fusion.4 = bf16[4,1536]{1,0:T(4,128)(2,1)S(1)} fusion(f32[4,1536,512]{1,2,0:T(8,128)} %get-tuple-element.16, f32[4,1536]{1,0:T(4,128)S(1)} %sub.72, s32[4,1536]{1,0:T(4,128)S(1)} %copy-done.6, f32[4,1536]{1,0:T(4,128)S(1)} %bitcast.71), kind=kLoop, calls=%fused_computation.12 | loop fusion | flops 18868224 | bytes 12668928 | tf_op jit(solution)/shard_map/reduce_sum | solution.py:298
  167.8 5.2 %fusion.29 = f32[4,1,768]{2,1,0:T(1,128)S(1)} fusion(bf16[4,1536,768]{2,1,0:T(8,128)(2,1)} %bitcast.58, bf16[4,1536,1]{1,0,2:T(4,128)(2,1)S(1)} %bitcast.73), kind=kOutput, calls=%fused_computation.59 | convolution fusion | flops 9437184 | bytes 9461760 | tf_op jit(solution)/shard_map/cs,csd->cd/dot_general | solution.py:318
  172.9 0.6 broadcast_in_dim.113
  173.6 4.9 %all-to-all-start.2 = ((f32[4,4,768]{2,1,0:T(4,128)}), f32[4,4,768]{2,1,0:T(4,128)S(1)}, u32[]{:S(2)}, u32[]{:S(2)}) async-start(f32[4,4,768]{2,1,0:T(4,128)} %broadcast_in_dim.113), calls=%async_computation.3 | async-start | bytes 98304 | tf_op jit(solution)/shard_map/all_to_all | solution.py:24
  178.5 12.5 %add_convert_fusion = bf16[4,1536,768]{2,1,0:T(8,128)(2,1)} fusion(f32[4,768]{1,0:T(4,128)S(1)} %copy-done.7, f32[4,1536]{1,0:T(4,128)S(1)} %convert_element_type.76, bf16[4,512,768]{2,1,0:T(8,128)(2,1)S(1)} %copy-done, f32[4,1536,512]{1,2,0:T(8,128)} %get-tuple-element.16, f32[4,1536]{1,0:T(4,128)S(1)} %sub.72, s32[4,1536]{1,0:T(4,128)S(1)} %copy-done.6, ...), kind=kOutput, calls=%fused_computation.1 | convolution fusion | flops 4864868352 | bytes 25276416 | tf_op jit(solution)/shard_map/csl,cld->csd/dot_general | solution.py:301
  190.9 10.2 %bitcast_convert_fusion.p = bf16[32,256,768]{2,1,0:T(8,128)(2,1)} fusion(bf16[4,32,48,768]{3,2,1,0:T(8,128)(2,1)} %bitcast.78, f32[4,32,256]{2,0,1:T(4,128)S(1)} %copy.74, pred[4,32,256]{2,0,1:T(4,128)(4,1)S(1)} %bitcast.65), kind=kOutput, calls=%fused_computation | convolution fusion | flops 2425356288 | bytes 22183936 | tf_op jit(solution)/shard_map/csri,csrd->sid/dot_general | solution.py:307
  201.1 44.0 %shard_map.85 = f32[256,768]{1,0:T(8,128)} custom-call(bf16[32,256,768]{2,1,0:T(8,128)(2,1)} %bitcast_convert_fusion.p), custom_call_target="tpu_custom_call" | custom-call | tf_op jit(solution)/shard_map/pallas_call | solution.py:214
  245.1 0.0 all-to-all-done.2
  245.1 24.5 %all-gather = f32[32,4,768]{2,1,0:T(4,128)S(1)} all-gather(f32[1,4,768]{2,1,0:T(4,128)S(1)} %bitcast.76), channel_id=1, replica_groups=mesh['dp'=4,'label'=32] {'label'}, dimensions={0}, use_global_device_ids=true | all-gather | bytes 405504 | tf_op jit(solution)/shard_map/all_gather | solution.py:320
  269.6 0.9 reshape.137
  270.5 2.4 convert_element_type.57
  272.9 2.1 copy.117
  (28 shorter events, 0.3 us)
Async XLA Ops:
  7.2 83.9 %copy-start = (bf16[4,512,768]{2,1,0:T(8,128)(2,1)S(1)}, bf16[4,512,768]{2,1,0:T(8,128)(2,1)}, u32[]{:S(2)}) copy-start(bf16[4,512,768]{2,1,0:T(8,128)(2,1)} %param.6) | copy-start | bytes 9437188
  12.4 62.9 %copy-start.1 = (pred[32,256,4]{1,2,0:T(4,128)(4,1)}, pred[32,256,4]{1,2,0:T(4,128)(4,1)S(1)}, u32[]{:S(2)}) copy-start(pred[32,256,4]{1,2,0:T(4,128)(4,1)S(1)} %fusion.20) | copy-start | bytes 98308
  15.2 87.6 %copy-start.5 = (s32[4,1536]{1,0:T(4,128)}, s32[4,1536]{1,0:T(4,128)S(1)}, u32[]{:S(2)}) copy-start(s32[4,1536]{1,0:T(4,128)S(1)} %sub.68) | copy-start | bytes 73732
  91.0 11.9 %copy-start.3 = (f32[4,1,1536]{2,0,1:T(4,128)}, f32[4,1,1536]{2,0,1:T(4,128)S(1)}, u32[]{:S(2)}) copy-start(f32[4,1,1536]{2,0,1:T(4,128)S(1)} %copy.112) | copy-start | bytes 73732
  110.9 11.4 %all-to-all-start = ((f32[32,1,576]{2,1,0:T(1,128)}), f32[32,1,576]{2,1,0:T(1,128)S(1)}, u32[]{:S(2)}, u32[]{:S(2)}) async-start(f32[32,1,576]{2,1,0:T(1,128)} %reshape.145), calls=%async_computation | async-start | bytes 163840 | tf_op jit(solution)/shard_map/all_to_all | solution.py:18
  115.0 155.5 %reduce-scatter.2.cloned.1.call-start = ((), (), s32[]{:S(2)}) async-start(), calls=%async_computation.4 | async-start | bytes 3932160 | tf_op jit(solution)/shard_map/reduce_scatter | solution.py:315
  148.1 12.9 %copy-start.4 = (f32[4,1,1536]{2,0,1:T(4,128)S(1)}, f32[4,1,1536]{2,0,1:T(4,128)}, u32[]{:S(2)}) copy-start(f32[4,1,1536]{2,0,1:T(4,128)} %copy-done.3) | copy-start | bytes 73732
  148.1 12.9 %copy-start.6 = (s32[4,1536]{1,0:T(4,128)S(1)}, s32[4,1536]{1,0:T(4,128)}, u32[]{:S(2)}) copy-start(s32[4,1536]{1,0:T(4,128)} %copy-done.5) | copy-start | bytes 73732
  161.0 17.5 %copy-start.7 = (f32[4,768]{1,0:T(4,128)S(1)}, f32[4,768]{1,0:T(4,128)}, u32[]{:S(2)}) copy-start(f32[4,768]{1,0:T(4,128)} %get-tuple-element.13) | copy-start | bytes 36868
  173.6 71.5 %all-to-all-start.2 = ((f32[4,4,768]{2,1,0:T(4,128)}), f32[4,4,768]{2,1,0:T(4,128)S(1)}, u32[]{:S(2)}, u32[]{:S(2)}) async-start(f32[4,4,768]{2,1,0:T(4,128)} %broadcast_in_dim.113), calls=%async_computation.3 | async-start | bytes 98304 | tf_op jit(solution)/shard_map/all_to_all | solution.py:24
  178.5 12.5 %copy-start.2 = (pred[32,256,4]{1,2,0:T(4,128)(4,1)S(1)}, pred[32,256,4]{1,2,0:T(4,128)(4,1)}, u32[]{:S(2)}) copy-start(pred[32,256,4]{1,2,0:T(4,128)(4,1)} %copy-done.1) | copy-start | bytes 98308
Sparse Core Ops, SparseCore 0:
  160.5 37.2 reduce-scatter.1

commit v3 on v2

v3 whole, which is shorter than its diff:
```python
import jax
import jax.numpy as jnp
from jax import lax
from jax.experimental import pallas as pl
from jax.experimental.pallas import tpu as pltpu
from jax.sharding import PartitionSpec as P

LEAF = 512
K = 16
BIG = 1e30

MESH = pl.DeviceIdType.MESH

def place():
    me = lax.axis_index("label")
    core = lax.rem(me, 2)
    x = lax.rem(me // 2, 4)
    y = me // 8
    a = x * (1 - core) + y * core
    b = y * (1 - core) + x * core
    return me, core, a, b

def index_of(core, a, b):
    x = a * (1 - core) + b * core
    y = b * (1 - core) + a * core
    return (y * 4 + x) * 2 + core

OFF = (0, 3, 1, 2)

class Links:
    def __init__(self, send, recv):
        self.me, self.core, self.a, self.b = place()
        self.send, self.recv, self.sent = send, recv, []
        c, a, b = self.core, self.a, self.b
        self.partner = self.me + 1 - 2 * c
        self.dev = {
            "a-": index_of(c, lax.rem(a + 3, 4), b),
            "a+": index_of(c, lax.rem(a + 1, 4), b),
            "b-": index_of(c, a, lax.rem(b + 3, 4)),
            "b+": index_of(c, a, lax.rem(b + 1, 4)),
            "p": self.partner,
        }
    def block(self, i, j):
        return index_of(self.core, lax.rem(self.a + OFF[i], 4), lax.rem(self.b + OFF[j], 4))
    def partner_block(self, i, j):
        return index_of(1 - self.core, lax.rem(self.b + OFF[i], 4), lax.rem(self.a + OFF[j], 4))
    def meet(self, peers=None):
        barrier = pltpu.get_barrier_semaphore()
        peers = list(self.dev.values()) if peers is None else peers
        for d in peers:
            pl.semaphore_signal(barrier, inc=1, device_id={"label": d}, device_id_type=MESH)
        pl.semaphore_wait(barrier, len(peers))
    def copy(self, src, dst, slot, to):
        n = len(self.sent)
        c = pltpu.make_async_remote_copy(src_ref=src, dst_ref=dst, send_sem=self.send.at[n],
            recv_sem=self.recv.at[slot], device_id={"label": self.dev[to]}, device_id_type=MESH)
        c.start()
        self.sent.append(c)
    def wait(self, dst, slot):
        pltpu.make_async_remote_copy(src_ref=dst, dst_ref=dst, send_sem=self.send.at[0],
            recv_sem=self.recv.at[slot], device_id={"label": self.partner}, device_id_type=MESH).wait_recv()
    def drain(self):
        for c in self.sent:
            c.wait_send()


SLOTS = 48


def slot_tables(ids, pos):
    f32 = jnp.float32
    n = ids.shape[1]
    rows = lax.broadcasted_iota(jnp.int32, ids.shape, 0)
    pos_cluster = jnp.sum(
        jnp.where(rows == (pos >> 9), ids, 0).astype(f32), axis=0, keepdims=True
    )
    line = lax.broadcasted_iota(jnp.int32, (8, n), 0)
    named = jnp.zeros((8, n), f32)
    for c in range(4):
        hit = jnp.sum((ids == c).astype(f32), axis=0, keepdims=True)
        named = jnp.where(line == c, hit, named)
    earlier = (
        lax.broadcasted_iota(jnp.int32, (n, n), 0) < lax.broadcasted_iota(jnp.int32, (n, n), 1)
    ).astype(f32)
    rank = jnp.dot(
        named.astype(jnp.bfloat16), earlier.astype(jnp.bfloat16), preferred_element_type=f32
    )
    code = jnp.where(named > 0.5, rank, -1.0)
    target = ((pos & (LEAF - 1)) + 1).astype(f32)
    targets = jnp.where(pos_cluster == (line - 4).astype(f32), target, 0.0)
    return jnp.where(line < 4, code, targets)


def picks(info, c):
    r = lax.broadcasted_iota(jnp.int32, (SLOTS, info.shape[1]), 0).astype(jnp.float32)
    return info[c : c + 1] == r


def target_column(info, pick, c):
    return jnp.sum(jnp.where(pick, info[4 + c : 5 + c], 0.0), axis=1, keepdims=True) - 1.0


def forward_kernel(q_ref, labels, match, ids_ref, pos_ref, scores_out, rec_out, info, lse, losses,
                   g, scores, rec, st, sr, send, recv, st_send, st_recv, lse_send, lse_recv, out_sem):
    f32 = jnp.float32
    L = Links(send, recv)
    peers = [(k, L.block(i, j)) for k, (i, j) in enumerate([(i, j) for i in range(4) for j in range(4)])]
    peers = [d for k, d in peers if k > 0]
    peers += [L.partner_block(i, j) for i in range(4) for j in range(4)]
    L.meet(peers)
    half = q_ref.shape[0] // 2
    first = L.me * 4
    lo = lambda k: g.at[k, pl.ds(0, half)]
    hi = lambda k: g.at[k, pl.ds(half, half)]
    own = L.block(0, 0)
    for to, slot in (("a+", 0), ("a-", 1), ("b+", 4), ("b-", 5), ("p", 20)):
        L.copy(q_ref, g.at[own], slot, to)
    g[own] = q_ref[...]

    def side_a(i):
        k = L.block(i, 0)
        L.wait(g.at[k], i - 1)
        if i == 1:
            L.copy(lo(k), lo(k), 2, "a+")
        else:
            L.copy(hi(k), hi(k), 3, "a-")
        L.copy(g.at[k], g.at[k], 4 + 4 * i, "b+")
        L.copy(g.at[k], g.at[k], 5 + 4 * i, "b-")
        L.copy(g.at[k], g.at[k], 20 + 4 * i, "p")

    def far_a():
        k = L.block(3, 0)
        L.wait(lo(k), 2)
        L.wait(hi(k), 3)
        L.copy(g.at[k], g.at[k], 16, "b+")
        L.copy(g.at[k], g.at[k], 17, "b-")
        L.copy(g.at[k], g.at[k], 32, "p")

    def side_b(i):
        k = L.block(i, 1)
        L.wait(g.at[k], 4 + 4 * i)
        L.copy(lo(k), lo(k), 6 + 4 * i, "b+")
        L.copy(g.at[k], g.at[k], 21 + 4 * i, "p")
        k = L.block(i, 2)
        L.wait(g.at[k], 5 + 4 * i)
        L.copy(hi(k), hi(k), 7 + 4 * i, "b-")
        L.copy(g.at[k], g.at[k], 22 + 4 * i, "p")

    def far_b(i):
        k = L.block(i, 3)
        L.wait(lo(k), 6 + 4 * i)
        L.wait(hi(k), 7 + 4 * i)
        L.copy(g.at[k], g.at[k], 23 + 4 * i, "p")
        for j in range(4):
            k = L.partner_block(i, j)
            L.wait(g.at[k], 20 + 4 * i + j)

    def work(i):
        def block_of(n):
            other, j = n // 4, lax.rem(n, 4)
            core = L.core + other - 2 * L.core * other
            a = lax.rem(L.a * (1 - other) + L.b * other + OFF[i], 4)
            return index_of(core, a, j)

        def pick(n, carry):
            s = block_of(n)
            table = slot_tables(ids_ref[s] - first, pos_ref[s])
            info[s] = table
            one = jnp.concatenate([picks(table, c).astype(f32) for c in range(4)], axis=0)
            rows = jnp.dot(one.astype(jnp.bfloat16), g[s], preferred_element_type=f32)
            rec[s] = rows.astype(jnp.bfloat16).reshape(4, SLOTS, rows.shape[1])
            return carry

        lax.fori_loop(0, 8, pick, 0)

        def score(c, carry):
            rows = jnp.concatenate([rec[block_of(n), c] for n in range(8)], axis=0)
            out = lax.dot_general(rows, labels[c], (((1,), (1,)), ((), ())), preferred_element_type=f32)
            bias = jnp.sum(rows.astype(f32) * match[c].astype(f32), axis=1, keepdims=True)
            out = out + bias
            for n in range(8):
                scores[block_of(n), c] = out[n * SLOTS : (n + 1) * SLOTS]
            return carry

        lax.fori_loop(0, 4, score, 0)

        def stat(n, carry):
            s = block_of(n)
            table = info[s]
            leaf = lax.broadcasted_iota(jnp.int32, (SLOTS, LEAF), 1).astype(f32)
            parts = []
            for c in range(4):
                one = picks(table, c)
                val = scores[s, c]
                top = jnp.max(val, axis=1, keepdims=True)
                total = jnp.sum(jnp.exp(val - top), axis=1, keepdims=True)
                picked = jnp.sum(
                    jnp.where(leaf == target_column(table, one, c), val, 0.0), axis=1, keepdims=True
                )
                parts.append((one, top, total, picked))
            best = jnp.full((1, table.shape[1]), -BIG, f32)
            for one, top, total, picked in parts:
                best = jnp.maximum(best, jnp.max(jnp.where(one, top, -BIG), axis=0, keepdims=True))
            spread = jnp.zeros_like(best)
            chosen = jnp.zeros_like(best)
            for one, top, total, picked in parts:
                spread += jnp.sum(
                    jnp.where(one, total * jnp.exp(jnp.where(one, top - best, 0.0)), 0.0), axis=0, keepdims=True
                )
                chosen += jnp.sum(jnp.where(one, picked, 0.0), axis=0, keepdims=True)
            line = lax.broadcasted_iota(jnp.int32, (8, table.shape[1]), 0)
            st[s] = jnp.where(line == 0, best, jnp.where(line == 1, spread, chosen))
            return carry

        lax.fori_loop(0, 8, stat, 0)
        for core in range(2):
            for j in range(4):
                k = L.block(i, j) if core == 0 else L.partner_block(i, j)
                n = 8 * i + 4 * core + j
                pltpu.make_async_copy(scores.at[k], scores_out.at[k], out_sem.at[2 * n]).start()
                pltpu.make_async_copy(rec.at[k], rec_out.at[k], out_sem.at[2 * n + 1]).start()
                if n == 0:
                    continue
                pltpu.make_async_remote_copy(
                    src_ref=st.at[k], dst_ref=sr.at[L.me], send_sem=st_send.at[k], recv_sem=st_recv.at[L.me],
                    device_id={"label": k}, device_id_type=MESH,
                ).start()

    side_a(1)
    side_a(2)
    side_b(0)
    far_a()
    side_b(1)
    far_b(0)
    work(0)
    side_b(2)
    far_b(1)
    work(1)
    side_b(3)
    far_b(2)
    work(2)
    far_b(3)
    work(3)
    sr[own] = st[own]

    def stat_copy(k, arrive):
        return pltpu.make_async_remote_copy(
            src_ref=st.at[k], dst_ref=sr.at[k], send_sem=st_send.at[k], recv_sem=st_recv.at[k],
            device_id={"label": k}, device_id_type=MESH,
        )

    for k in peers:
        stat_copy(k, True).wait_recv()
    best = jnp.max(sr[:, 0:1, :], axis=0)
    lines = sr[...]
    spread = jnp.sum(lines[:, 1:2, :] * jnp.exp(lines[:, 0:1, :] - best[None]), axis=0)
    chosen = jnp.sum(lines[:, 2:3, :], axis=0)
    value = best + jnp.log(spread)
    losses[...] = jnp.broadcast_to(value - chosen, losses.shape)
    lse[own] = jnp.broadcast_to(value, lse.shape[1:])

    def lse_copy(dev, row):
        return pltpu.make_async_remote_copy(
            src_ref=lse.at[row], dst_ref=lse.at[row], send_sem=lse_send.at[dev], recv_sem=lse_recv.at[row],
            device_id={"label": dev}, device_id_type=MESH,
        )

    for k in peers:
        lse_copy(k, own).start()
    for k in peers:
        lse_copy(k, k).wait_recv()
    for k in peers:
        stat_copy(k, False).wait_send()
        lse_copy(k, own).wait_send()
    for i in range(4):
        for core in range(2):
            for j in range(4):
                k = L.block(i, j) if core == 0 else L.partner_block(i, j)
                n = 8 * i + 4 * core + j
                pltpu.make_async_copy(scores.at[k], scores_out.at[k], out_sem.at[2 * n]).wait()
                pltpu.make_async_copy(rec.at[k], rec_out.at[k], out_sem.at[2 * n + 1]).wait()
    L.drain()


def forward(q, labels, match, ids, pos):
    q_dev, width = q.shape
    vmem = pl.BlockSpec(memory_space=pltpu.VMEM)
    hbm = pl.BlockSpec(memory_space=pl.ANY)
    shape = jax.ShapeDtypeStruct
    f32, bf16, dma = jnp.float32, jnp.bfloat16, pltpu.SemaphoreType.DMA
    return pl.pallas_call(
        forward_kernel,
        out_shape=(
            shape((32, 4, SLOTS, LEAF), f32),
            shape((32, 4, SLOTS, width), bf16),
            shape((32, 8, q_dev), f32),
            shape((32, 8, q_dev), f32),
            shape((8, q_dev), f32),
        ),
        in_specs=[vmem] * 5,
        out_specs=(hbm, hbm, vmem, vmem, vmem),
        scratch_shapes=[
            pltpu.VMEM((32, q_dev, width), bf16),
            pltpu.VMEM((32, 4, SLOTS, LEAF), f32),
            pltpu.VMEM((32, 4, SLOTS, width), bf16),
            pltpu.VMEM((32, 8, q_dev), f32),
            pltpu.VMEM((32, 8, q_dev), f32),
            dma((36,)), dma((36,)), dma((32,)), dma((32,)), dma((32,)), dma((32,)), dma((64,)),
        ],
        compiler_params=pltpu.CompilerParams(
            collective_id=0, has_side_effects=True, vmem_limit_bytes=60 * 1024 * 1024
        ),
    )(q, labels, match, ids, pos)


def backward_kernel(scores, rec, info, lse, labels, match, partial, label_part, local_sum,
                    delta, coef, grads, held):
    f32, bf16 = jnp.float32, jnp.bfloat16
    step = pl.program_id(0)
    blocks = scores.shape[0]

    @pl.when(step == 0)
    def _():
        local_sum[...] = jnp.zeros_like(local_sum)

    def part(n, carry):
        table = info[n]
        leaf = lax.broadcasted_iota(jnp.int32, (SLOTS, LEAF), 1).astype(f32)
        log_sum = lse[n, 0:1]
        for c in range(4):
            one = picks(table, c)
            used = jnp.sum(jnp.where(one, 1.0, 0.0), axis=1, keepdims=True) > 0.5
            norm = jnp.sum(jnp.where(one, log_sum, 0.0), axis=1, keepdims=True)
            norm = jnp.where(used, norm, BIG)
            hit = leaf == target_column(table, one, c)
            value = jnp.exp(scores[n, c] - norm) - hit.astype(f32)
            total = jnp.sum(value, axis=1, keepdims=True).astype(bf16)
            rows = pl.ds(pl.multiple_of((step * blocks + n) * SLOTS, 16), SLOTS)
            delta[c, rows] = value.astype(bf16)
            coef[c, pl.ds(pl.multiple_of(n * SLOTS, 16), SLOTS)] = jnp.broadcast_to(total.astype(f32), (SLOTS, 128))
            local_sum[c] += jnp.sum(total.astype(f32) * rec[n, c].astype(f32), axis=0, keepdims=True)
        return carry

    lax.fori_loop(0, blocks, part, 0)

    def slot(c, carry):
        rows = pl.ds(pl.multiple_of(step * blocks * SLOTS, 16), blocks * SLOTS)
        out = jnp.dot(delta[c, rows], labels[c], preferred_element_type=f32)
        out = out + coef[c][:, 0:1] * match[c].astype(f32)
        out = out.astype(bf16)
        for n in range(blocks):
            grads[n, pl.ds(pl.multiple_of(c * SLOTS, 16), SLOTS)] = out[n * SLOTS : (n + 1) * SLOTS]
        return carry

    lax.fori_loop(0, 4, slot, 0)

    def back(n, carry):
        table = info[n]
        one = jnp.concatenate([picks(table, c).astype(f32) for c in range(4)], axis=0).astype(bf16)
        out = lax.dot_general(one, grads[n], (((0,), (0,)), ((), ())), preferred_element_type=f32)
        partial[n] = out.astype(bf16)
        return carry

    lax.fori_loop(0, blocks, back, 0)

    for n in range(blocks):
        held[:, pl.ds(pl.multiple_of((step * blocks + n) * SLOTS, 16), SLOTS)] = rec[n]

    @pl.when(step == pl.num_programs(0) - 1)
    def _():
        def gather_part(c, carry):
            out = lax.dot_general(delta[c], held[c], (((0,), (0,)), ((), ())), preferred_element_type=f32)
            label_part[c] = out.astype(bf16)
            return carry

        lax.fori_loop(0, 4, gather_part, 0)


def backward(scores, rec, info, lse, labels, match):
    n, _, _, width = rec.shape
    q_dev = info.shape[2]
    f32, bf16 = jnp.float32, jnp.bfloat16
    group = 8
    vmem = pl.BlockSpec(memory_space=pltpu.VMEM)
    shape = jax.ShapeDtypeStruct
    return pl.pallas_call(
        backward_kernel,
        grid=(n // group,),
        out_shape=(
            shape((n, q_dev, width), bf16),
            shape((4, LEAF, width), bf16),
            shape((4, 1, width), f32),
        ),
        in_specs=[
            pl.BlockSpec((group, 4, SLOTS, LEAF), lambda i: (i, 0, 0, 0)),
            pl.BlockSpec((group, 4, SLOTS, width), lambda i: (i, 0, 0, 0)),
            pl.BlockSpec((group, 8, q_dev), lambda i: (i, 0, 0)),
            pl.BlockSpec((group, 8, q_dev), lambda i: (i, 0, 0)),
            vmem,
            vmem,
        ],
        out_specs=(
            pl.BlockSpec((group, q_dev, width), lambda i: (i, 0, 0)),
            vmem,
            vmem,
        ),
        scratch_shapes=[
            pltpu.VMEM((4, n * SLOTS, LEAF), bf16),
            pltpu.VMEM((4, group * SLOTS, 128), f32),
            pltpu.VMEM((group, 4 * SLOTS, width), bf16),
            pltpu.VMEM((4, n * SLOTS, width), bf16),
        ],
        compiler_params=pltpu.CompilerParams(vmem_limit_bytes=60 * 1024 * 1024),
    )(scores, rec, info, lse, labels, match)


def scatter_kernel(p, out, t, u, pr, bh, bf, ah, af, send, recv):
    L = Links(send, recv)
    L.meet()
    half = p.shape[1] // 2
    f32 = jnp.float32
    ORDER = [(i, 3) for i in (3, 1, 2, 0)] + [(i, j) for i in (3, 1, 2, 0) for j in (1, 2)] + [(i, 0) for i in (3, 1, 2, 0)]
    for i, j in ORDER:
        L.copy(p.at[L.partner_block(i, j)], pr.at[4 * i + j], 4 * i + j, "p")
    LO, HI = pl.ds(0, half), pl.ds(half, half)
    def both(i, j):
        L.wait(pr.at[4 * i + j], 4 * i + j)
        return lambda s: p[L.block(i, j), s].astype(f32) + pr[4 * i + j, s].astype(f32)
    for i in (3, 1, 2, 0):
        s = both(i, 3)
        n = 3 * i + 2
        t[n] = s(slice(None)).astype(t.dtype)
        L.copy(t.at[n, LO], bh.at[i, 0], 16 + 4 * i, "b+")
        L.copy(t.at[n, HI], bh.at[i, 1], 17 + 4 * i, "b-")
    for i in (3, 1, 2, 0):
        s = both(i, 2)
        n = 3 * i + 1
        L.wait(bh.at[i, 0], 16 + 4 * i)
        t[n, LO] = (s(LO) + bh[i, 0].astype(f32)).astype(t.dtype)
        t[n, HI] = s(HI).astype(t.dtype)
        L.copy(t.at[n], bf.at[i, 0], 18 + 4 * i, "b+")
        s = both(i, 1)
        n = 3 * i
        L.wait(bh.at[i, 1], 17 + 4 * i)
        t[n, HI] = (s(HI) + bh[i, 1].astype(f32)).astype(t.dtype)
        t[n, LO] = s(LO).astype(t.dtype)
        L.copy(t.at[n], bf.at[i, 1], 19 + 4 * i, "b-")
    def column(i):
        s = both(i, 0)
        L.wait(bf.at[i, 0], 18 + 4 * i)
        L.wait(bf.at[i, 1], 19 + 4 * i)
        return lambda r: s(r) + bf[i, 0, r].astype(f32) + bf[i, 1, r].astype(f32)
    s = column(3)
    u[2] = s(slice(None)).astype(u.dtype)
    L.copy(u.at[2, LO], ah.at[0], 32, "a+")
    L.copy(u.at[2, HI], ah.at[1], 33, "a-")
    s = column(1)
    L.wait(ah.at[1], 33)
    u[0, HI] = (s(HI) + ah[1].astype(f32)).astype(u.dtype)
    u[0, LO] = s(LO).astype(u.dtype)
    L.copy(u.at[0], af.at[1], 35, "a-")
    s = column(2)
    L.wait(ah.at[0], 32)
    u[1, LO] = (s(LO) + ah[0].astype(f32)).astype(u.dtype)
    u[1, HI] = s(HI).astype(u.dtype)
    L.copy(u.at[1], af.at[0], 34, "a+")
    s = column(0)
    L.wait(af.at[0], 34)
    L.wait(af.at[1], 35)
    out[...] = s(slice(None)) + af[0].astype(f32) + af[1].astype(f32)
    L.drain()

def scatter(p):
    n, r, w = p.shape
    bf16 = jnp.bfloat16
    return pl.pallas_call(
        scatter_kernel,
        out_shape=jax.ShapeDtypeStruct((r, w), jnp.float32),
        in_specs=[pl.BlockSpec(memory_space=pltpu.VMEM)],
        out_specs=pl.BlockSpec(memory_space=pltpu.VMEM),
        scratch_shapes=[pltpu.VMEM((12, r, w), bf16), pltpu.VMEM((3, r, w), bf16), pltpu.VMEM((16, r, w), bf16),
            pltpu.VMEM((4, 2, r // 2, w), bf16), pltpu.VMEM((4, 2, r, w), bf16), pltpu.VMEM((2, r // 2, w), bf16), pltpu.VMEM((2, r, w), bf16),
            pltpu.SemaphoreType.DMA((36,)), pltpu.SemaphoreType.DMA((36,))],
        compiler_params=pltpu.CompilerParams(collective_id=1, has_side_effects=True),
    )(p)


def over_copies(shard, axis):
    devices = lax.axis_size(axis)
    spread = jnp.broadcast_to(shard[None], (devices, *shard.shape))
    return lax.all_to_all(spread, axis, 0, 0, tiled=True).sum(axis=0)


def body(queries, labels, matcher, cluster_ids, positives):
    q_dev, width = queries.shape
    cl_dev = labels.shape[0]
    n_label = lax.axis_size("label")
    first = lax.axis_index("label") * cl_dev
    match = lax.dynamic_slice_in_dim(matcher, first, cl_dev, 0).reshape(cl_dev, 1, width)
    ids = cluster_ids.reshape(n_label, q_dev, K).transpose(0, 2, 1)
    pos = positives.reshape(n_label, 1, q_dev)
    scores, received, info, lse, losses = forward(queries, labels, match, ids, pos)
    partial, label_part, local_sum = backward(scores, received, info, lse, labels, match)
    label_grads = lax.psum_scatter(
        label_part, "dp", scatter_dimension=1, tiled=True
    ).astype(jnp.float32)
    query_grads = scatter(partial)
    local_sum = over_copies(local_sum.reshape(cl_dev, width), "dp")
    matcher_grads = lax.all_gather(local_sum, "label", axis=0, tiled=True)
    return (losses[0], query_grads, label_grads, matcher_grads)


def solution(mesh):
    return jax.shard_map(
        body,
        mesh=mesh,
        in_specs=(P(("dp", "label"), None), P("label", None, None), P(), P("dp", None), P("dp")),
        out_specs=(P(("dp", "label")), P(("dp", "label"), None), P("label", "dp", None), P()),
        check_vma=False,
    )
```

time: 283 us -> 228 us (0.81)
  Pallas kernels: 93.2 us -> 172 us
  matrix products: 69.3 us -> 0 us
  other arithmetic: 37.1 us -> 2.43 us
  blocking collectives: 36.7 us -> 24.2 us
  local copies, waits for them, and re-layouts: 19.9 us -> 8.94 us
  starting transfers between devices: 9.02 us -> 5.07 us
    pallas_call x1 -> x2, Pallas kernels: 49.3 us -> 128 us  [the longest x1 87 us: forward(): pl.pallas_call(forward_kernel, out_shape=(shape((32, 4, SLOTS, LEAF), f32...]
    dot_general x9 -> x0, matrix products: 69.3 us -> none  [the longest x1 12.5 us: body(): jnp.einsum('csl,cld->csd', delta_b, labels, preferred_element_type=jnp.fl...]
    reduce_sum x7 -> x1, other arithmetic: 23.6 us -> 0.02 us  [over_copies(): return lax.all_to_all(spread, axis, 0, 0, tiled=True).sum(axis=0)]
    all_to_all x1 -> x0, blocking collectives: 12.2 us -> none  [body(): lax.all_to_all(outgoing_lse, 'label', split_axis=1, concat_axis=1, tiled=...]
    convert_element_type x1 -> x0, local copies, waits for them, and re-layouts: 8.12 us -> none  [body(): received = picked_rows.astype(jnp.bfloat16).reshape(cl_dev, rows_dev, width)]
    reduce_or x3 -> x0, other arithmetic: 4.3 us -> none  [the longest x1 2.27 us: body(): used = jnp.any(select_own, axis=3)]
    all_to_all x2 -> x1, starting transfers between devices: 8.98 us -> 5.03 us  [over_copies(): return lax.all_to_all(spread, axis, 0, 0, tiled=True).sum(axis=0)]
    unnamed x22 -> x5, local copies, waits for them, and re-layouts: 5.75 us -> 4.53 us
  transfers between devices with their start and end apart: 3 -> 2, of which waited for: 1 -> 0; matrix products, arithmetic and copies ran while one was open for 15% -> 2% of each run, Pallas kernels for 16% -> 20%
where the time goes in v3:
time: 228 us; the launch traced here: 227 us
  Pallas kernels  172 us (75%)
  blocking collectives  24.2 us (11%)
  between operations  14.1 us (6%)
  local copies, waits for them, and re-layouts  8.94 us (4%)
  starting transfers between devices  5.07 us (2%)
  other arithmetic  2.43 us (1%)
    pallas_call x1, Pallas kernels, forward(): pl.pallas_call(forward_kernel, out_shape=(shape((32, 4, SLOTS, LEAF), f32...  87 us
    pallas_call x1, Pallas kernels, scatter(): pl.pallas_call(scatter_kernel, out_shape=jax.ShapeDtypeStruct((r, w), jnp...  44.4 us
    pallas_call x1, Pallas kernels, backward(): pl.pallas_call(backward_kernel, grid=(n // group,), out_shape=(shape((n,...  41 us
    all_gather x1, blocking collectives, body(): matcher_grads = lax.all_gather(local_sum, 'label', axis=0, tiled=True)  24.2 us
    all_to_all x1, starting transfers between devices, over_copies(): return lax.all_to_all(spread, axis, 0, 0, tiled=True).sum(axis=0)  5.03 us
  transfers between devices with their start and end apart: 2, of which 0 were waited for; matrix products, arithmetic and copies ran while one was open for 2% of the time, Pallas kernels for 20%

profile of v3, /device:TPU:1, one launch (start us, length us, event | category | flops | bytes accessed | tf_op | source)
XLA Modules:
  0.0 227.2 jit_solution(18143341309035403702)
XLA Ops:
  7.2 0.0 copy-start
  7.2 0.0 reduce-scatter.2.cloned.1.call-start
  7.2 0.9 copy-done
  8.1 0.6 copy.16.match
  8.7 1.9 copy.22
  10.6 87.0 %shard_map.84 = (f32[32,4,48,512]{3,2,1,0:T(8,128)}, bf16[32,4,48,768]{3,2,1,0:T(8,128)(2,1)}, f32[32,8,256]{2,1,0:T(8,128)}, f32[32,8,256]{2,1,0:T(8,128)}, f32[8,256]{1,0:T(8,128)}) custom-call(bf16[256,768]{1,0:T(8,128)(2,1)} %q_ref.1, bf16[4,512,768]{2,1,0:T(8,128)(2,1)} %labels.3, bf16[4,1,768]{2,1,0:T(2,128)(2,1)} %copy.16.match, ...), custom_call_target="tpu_custom_call" | custom-call | tf_op jit(solution)/shard_map/pallas_call | solution.py:291
  97.6 41.0 %shard_map.85 = (bf16[32,256,768]{2,1,0:T(8,128)(2,1)}, bf16[4,512,768]{2,1,0:T(8,128)(2,1)}, f32[4,1,768]{2,1,0:T(1,128)}) custom-call(f32[32,4,48,512]{3,2,1,0:T(8,128)} %get-tuple-element.13.scores, bf16[32,4,48,768]{3,2,1,0:T(8,128)(2,1)} %get-tuple-element.14.rec, f32[32,8,256]{2,1,0:T(8,128)} %get-tuple-element.15.info, ...), custom_call_target="tpu_custom_call" | custom-call | tf_op jit(solution)/shard_map/pallas_call | solution.py:386
  138.7 0.0 reduce-scatter.2.cloned.1.call-update
  138.7 0.7 copy.23
  139.4 0.6 broadcast_in_dim.8
  140.0 5.0 %all-to-all-start = ((f32[4,4,768]{2,1,0:T(4,128)}), f32[4,4,768]{2,1,0:T(4,128)S(1)}, u32[]{:S(2)}, u32[]{:S(2)}) async-start(f32[4,4,768]{2,1,0:T(4,128)} %broadcast_in_dim.8), calls=%async_computation.1 | async-start | bytes 98304 | tf_op jit(solution)/shard_map/all_to_all | solution.py:491
  145.1 1.3 slice.3
  146.3 44.4 %shard_map.86 = f32[256,768]{1,0:T(8,128)} custom-call(bf16[32,256,768]{2,1,0:T(8,128)(2,1)} %get-tuple-element.17.p), custom_call_target="tpu_custom_call" | custom-call | tf_op jit(solution)/shard_map/pallas_call | solution.py:476
  190.8 0.0 all-to-all-done
  190.8 24.2 %all-gather = f32[32,4,768]{2,1,0:T(4,128)S(1)} all-gather(f32[1,4,768]{2,1,0:T(4,128)S(1)} %bitcast.17), channel_id=1, replica_groups=mesh['dp'=4,'label'=32] {'label'}, dimensions={0}, use_global_device_ids=true | all-gather | bytes 405504 | tf_op jit(solution)/shard_map/all_gather | solution.py:509
  215.0 0.9 reshape.22
  215.9 0.0 reduce-scatter.2.cloned.1.call-done
  215.9 2.4 %convert_element_type.3 = f32[4,128,768]{2,1,0:T(8,128)} convert(bf16[4,128,768]{2,1,0:T(8,128)(2,1)} %reduce-scatter.2.cloned.1.call-done) | non-fusion elementwise | flops 393216 | bytes 2359296 | tf_op jit(solution)/shard_map/convert_element_type | solution.py:506
  218.3 2.1 copy.25
  (2 shorter events, 0.0 us)
Async XLA Ops:
  7.2 0.9 copy-start
  7.2 208.7 %reduce-scatter.2.cloned.1.call-start = ((), (), s32[]{:S(2)}) async-start(), calls=%async_computation.2 | async-start | bytes 3932160 | tf_op jit(solution)/shard_map/reduce_scatter | solution.py:504
  140.0 50.7 %all-to-all-start = ((f32[4,4,768]{2,1,0:T(4,128)}), f32[4,4,768]{2,1,0:T(4,128)S(1)}, u32[]{:S(2)}, u32[]{:S(2)}) async-start(f32[4,4,768]{2,1,0:T(4,128)} %broadcast_in_dim.8), calls=%async_computation.1 | async-start | bytes 98304 | tf_op jit(solution)/shard_map/all_to_all | solution.py:491
Sparse Core Ops, SparseCore 0:
  138.8 37.9 reduce-scatter.1

commit v4 on v3

--- a/solution.py
+++ b/solution.py
@@ -414,42 +414,106 @@
     )(scores, rec, info, lse, labels, match)
 
 
-def scatter_kernel(p, out, t, u, pr, bh, bf, ah, af, send, recv):
+class Column:
+    def __init__(self, links):
+        self.z = lax.axis_index("dp")
+        self.links = links
+
+    def copy(self, src, dst, slot, off):
+        L = self.links
+        n = len(L.sent)
+        c = pltpu.make_async_remote_copy(
+            src_ref=src, dst_ref=dst, send_sem=L.send.at[n], recv_sem=L.recv.at[slot],
+            device_id={"dp": lax.rem(self.z + off, 4)}, device_id_type=MESH,
+        )
+        c.start()
+        L.sent.append(c)
+
+
+def scatter_kernel(p, lp, ls, out, label_out, mout, t_all, u, pr, bh, bf, ah, af, zt, zh, zf, mz, send, recv, m_recv):
     L = Links(send, recv)
-    L.meet()
+    Z = Column(L)
+    z = Z.z
+    peers = [L.block(i, j) for i in range(4) for j in range(4)][1:]
+    peers += [L.partner_block(i, j) for i in range(4) for j in range(4)]
+    barrier = pltpu.get_barrier_semaphore()
+    for d in peers:
+        pl.semaphore_signal(barrier, inc=1, device_id={"label": d}, device_id_type=MESH)
+    for off in (1, 2, 3):
+        pl.semaphore_signal(barrier, inc=1, device_id={"dp": lax.rem(z + off, 4)}, device_id_type=MESH)
+    pl.semaphore_wait(barrier, 34)
     half = p.shape[1] // 2
     f32 = jnp.float32
+    rows_z = label_out.shape[1]
+
+    def rows(off):
+        return pl.ds(pl.multiple_of(lax.rem(z + off, 4) * rows_z, rows_z), rows_z)
+
+    PAIRS = pl.ds(0, 2), pl.ds(2, 2)
+    for off in (1, 2, 3):
+        Z.copy(ls.at[lax.rem(z + off, 4)], mz.at[z], 41 + off, off)
     ORDER = [(i, 3) for i in (3, 1, 2, 0)] + [(i, j) for i in (3, 1, 2, 0) for j in (1, 2)] + [(i, 0) for i in (3, 1, 2, 0)]
     for i, j in ORDER:
         L.copy(p.at[L.partner_block(i, j)], pr.at[4 * i + j], 4 * i + j, "p")
+    Z.copy(lp.at[PAIRS[0], rows(2)], zh.at[0], 36, 1)
+    Z.copy(lp.at[PAIRS[1], rows(2)], zh.at[1], 37, 3)
     LO, HI = pl.ds(0, half), pl.ds(half, half)
+    mz[z] = ls[z]
+
     def both(i, j):
         L.wait(pr.at[4 * i + j], 4 * i + j)
         return lambda s: p[L.block(i, j), s].astype(f32) + pr[4 * i + j, s].astype(f32)
+
     for i in (3, 1, 2, 0):
         s = both(i, 3)
-        n = 3 * i + 2
-        t[n] = s(slice(None)).astype(t.dtype)
-        L.copy(t.at[n, LO], bh.at[i, 0], 16 + 4 * i, "b+")
-        L.copy(t.at[n, HI], bh.at[i, 1], 17 + 4 * i, "b-")
+        t = t_all.at[3 * i + 2]
+        t[...] = s(slice(None)).astype(t.dtype)
+        L.copy(t.at[LO], bh.at[i, 0], 16 + 4 * i, "b+")
+        L.copy(t.at[HI], bh.at[i, 1], 17 + 4 * i, "b-")
+    for off in (1, 2, 3):
+        L.wait(mz.at[lax.rem(z + 4 - off, 4)], 41 + off)
+    mout[z, L.me] = mz[0] + mz[1] + mz[2] + mz[3]
+
+    def row_copy(dev, row):
+        return pltpu.make_async_remote_copy(
+            src_ref=mout.at[z, row], dst_ref=mout.at[z, row], send_sem=m_recv.at[1, dev], recv_sem=m_recv.at[0, row],
+            device_id={"label": dev}, device_id_type=MESH,
+        )
+
+    for k in peers:
+        row_copy(k, L.me).start()
+    L.wait(zh.at[0], 36)
+    zt[1, 0:2] = (lp[PAIRS[0], rows(1)].astype(f32) + zh[0].astype(f32)).astype(zt.dtype)
+    zt[1, 2:4] = lp[PAIRS[1], rows(1)]
+    Z.copy(zt.at[1], zf.at[0], 38, 1)
+    L.wait(zh.at[1], 37)
+    zt[0, 2:4] = (lp[PAIRS[1], rows(3)].astype(f32) + zh[1].astype(f32)).astype(zt.dtype)
+    zt[0, 0:2] = lp[PAIRS[0], rows(3)]
+    Z.copy(zt.at[0], zf.at[1], 39, 3)
     for i in (3, 1, 2, 0):
         s = both(i, 2)
-        n = 3 * i + 1
+        t = t_all.at[3 * i + 1]
         L.wait(bh.at[i, 0], 16 + 4 * i)
-        t[n, LO] = (s(LO) + bh[i, 0].astype(f32)).astype(t.dtype)
-        t[n, HI] = s(HI).astype(t.dtype)
-        L.copy(t.at[n], bf.at[i, 0], 18 + 4 * i, "b+")
+        t[LO] = (s(LO) + bh[i, 0].astype(f32)).astype(t.dtype)
+        t[HI] = s(HI).astype(t.dtype)
+        L.copy(t, bf.at[i, 0], 18 + 4 * i, "b+")
         s = both(i, 1)
-        n = 3 * i
+        t = t_all.at[3 * i + 0]
         L.wait(bh.at[i, 1], 17 + 4 * i)
-        t[n, HI] = (s(HI) + bh[i, 1].astype(f32)).astype(t.dtype)
-        t[n, LO] = s(LO).astype(t.dtype)
-        L.copy(t.at[n], bf.at[i, 1], 19 + 4 * i, "b-")
+        t[HI] = (s(HI) + bh[i, 1].astype(f32)).astype(t.dtype)
+        t[LO] = s(LO).astype(t.dtype)
+        L.copy(t, bf.at[i, 1], 19 + 4 * i, "b-")
+    for k in peers:
+        row_copy(k, k).wait_recv()
+    for off in (1, 2, 3):
+        Z.copy(mout.at[z], mout.at[z], 44 + off, off)
+
     def column(i):
         s = both(i, 0)
         L.wait(bf.at[i, 0], 18 + 4 * i)
         L.wait(bf.at[i, 1], 19 + 4 * i)
         return lambda r: s(r) + bf[i, 0, r].astype(f32) + bf[i, 1, r].astype(f32)
+
     s = column(3)
     u[2] = s(slice(None)).astype(u.dtype)
     L.copy(u.at[2, LO], ah.at[0], 32, "a+")
@@ -464,31 +528,51 @@
     u[1, LO] = (s(LO) + ah[0].astype(f32)).astype(u.dtype)
     u[1, HI] = s(HI).astype(u.dtype)
     L.copy(u.at[1], af.at[0], 34, "a+")
+    L.wait(zf.at[0], 38)
+    L.wait(zf.at[1], 39)
+    label_out[...] = lp[:, rows(0)].astype(f32) + zf[0].astype(f32) + zf[1].astype(f32)
     s = column(0)
     L.wait(af.at[0], 34)
     L.wait(af.at[1], 35)
     out[...] = s(slice(None)) + af[0].astype(f32) + af[1].astype(f32)
+    for off in (1, 2, 3):
+        L.wait(mout.at[lax.rem(z + 4 - off, 4)], 44 + off)
+    for k in peers:
+        row_copy(k, L.me).wait_send()
     L.drain()
 
-def scatter(p):
+
+def scatter(p, lp, ls):
     n, r, w = p.shape
-    bf16 = jnp.bfloat16
+    clusters, leaf, _ = lp.shape
+    f32, bf16, dma = jnp.float32, jnp.bfloat16, pltpu.SemaphoreType.DMA
+    vmem = pl.BlockSpec(memory_space=pltpu.VMEM)
+    shape = jax.ShapeDtypeStruct
     return pl.pallas_call(
         scatter_kernel,
-        out_shape=jax.ShapeDtypeStruct((r, w), jnp.float32),
-        in_specs=[pl.BlockSpec(memory_space=pltpu.VMEM)],
-        out_specs=pl.BlockSpec(memory_space=pltpu.VMEM),
-        scratch_shapes=[pltpu.VMEM((12, r, w), bf16), pltpu.VMEM((3, r, w), bf16), pltpu.VMEM((16, r, w), bf16),
-            pltpu.VMEM((4, 2, r // 2, w), bf16), pltpu.VMEM((4, 2, r, w), bf16), pltpu.VMEM((2, r // 2, w), bf16), pltpu.VMEM((2, r, w), bf16),
-            pltpu.SemaphoreType.DMA((36,)), pltpu.SemaphoreType.DMA((36,))],
-        compiler_params=pltpu.CompilerParams(collective_id=1, has_side_effects=True),
-    )(p)
-
-
-def over_copies(shard, axis):
-    devices = lax.axis_size(axis)
-    spread = jnp.broadcast_to(shard[None], (devices, *shard.shape))
-    return lax.all_to_all(spread, axis, 0, 0, tiled=True).sum(axis=0)
+        out_shape=(shape((r, w), f32), shape((clusters, leaf // 4, w), f32), shape((4, n, 1, w), f32)),
+        in_specs=[vmem] * 3,
+        out_specs=(vmem,) * 3,
+        scratch_shapes=[
+            pltpu.VMEM((12, r, w), bf16),
+            pltpu.VMEM((3, r, w), bf16),
+            pltpu.VMEM((16, r, w), bf16),
+            pltpu.VMEM((4, 2, r // 2, w), bf16),
+            pltpu.VMEM((4, 2, r, w), bf16),
+            pltpu.VMEM((2, r // 2, w), bf16),
+            pltpu.VMEM((2, r, w), bf16),
+            pltpu.VMEM((2, clusters, leaf // 4, w), bf16),
+            pltpu.VMEM((2, 2, leaf // 4, w), bf16),
+            pltpu.VMEM((2, clusters, leaf // 4, w), bf16),
+            pltpu.VMEM((4, 1, w), f32),
+            dma((52,)),
+            dma((48,)),
+            dma((2, 32)),
+        ],
+        compiler_params=pltpu.CompilerParams(
+            collective_id=1, has_side_effects=True, vmem_limit_bytes=60 * 1024 * 1024
+        ),
+    )(p, lp, ls)
 
 
 def body(queries, labels, matcher, cluster_ids, positives):
@@ -501,12 +585,8 @@
     pos = positives.reshape(n_label, 1, q_dev)
     scores, received, info, lse, losses = forward(queries, labels, match, ids, pos)
     partial, label_part, local_sum = backward(scores, received, info, lse, labels, match)
-    label_grads = lax.psum_scatter(
-        label_part, "dp", scatter_dimension=1, tiled=True
-    ).astype(jnp.float32)
-    query_grads = scatter(partial)
-    local_sum = over_copies(local_sum.reshape(cl_dev, width), "dp")
-    matcher_grads = lax.all_gather(local_sum, "label", axis=0, tiled=True)
+    query_grads, label_grads, rows = scatter(partial, label_part, local_sum)
+    matcher_grads = rows.transpose(1, 0, 2, 3).reshape(matcher.shape)
     return (losses[0], query_grads, label_grads, matcher_grads)
 
 

time: 228 us -> 192 us (0.84)
  blocking collectives: 24.2 us -> 0 us
  between operations: 14.1 us -> 0.68 us
  Pallas kernels: 172 us -> 180 us
  starting transfers between devices: 5.07 us -> 0 us
  other arithmetic: 2.43 us -> 0 us
    all_gather x1 -> x0, blocking collectives: 24.2 us -> none  [body(): matcher_grads = lax.all_gather(local_sum, 'label', axis=0, tiled=True)]
    pallas_call x1, Pallas kernels: 44.4 us -> 51.8 us  [scatter(): pl.pallas_call(scatter_kernel, out_shape=(shape((r, w), f32), shape((clus...]
    all_to_all x1 -> x0, starting transfers between devices: 5.03 us -> none  [over_copies(): return lax.all_to_all(spread, axis, 0, 0, tiled=True).sum(axis=0)]
    convert_element_type x1 -> x0, other arithmetic: 2.41 us -> none  [body(): label_grads = lax.psum_scatter(label_part, 'dp', scatter_dimension=1, til...]
  transfers between devices with their start and end apart: 2 -> 0, of which waited for: 0 -> 0; matrix products, arithmetic and copies ran while one was open for 2% -> 0% of each run, Pallas kernels for 20% -> 0%
where the time goes in v4:
time: 192 us; the launch traced here: 191 us
  Pallas kernels  180 us (94%)
  local copies, waits for them, and re-layouts  10.2 us (5%)
    pallas_call x1, Pallas kernels, forward(): pl.pallas_call(forward_kernel, out_shape=(shape((32, 4, SLOTS, LEAF), f32...  87 us
    pallas_call x1, Pallas kernels, scatter(): pl.pallas_call(scatter_kernel, out_shape=(shape((r, w), f32), shape((clus...  51.8 us
    pallas_call x1, Pallas kernels, backward(): pl.pallas_call(backward_kernel, grid=(n // group,), out_shape=(shape((n,...  41 us
    unnamed x6, local copies, waits for them, and re-layouts  4.13 us

profile of v4, /device:TPU:1, one launch (start us, length us, event | category | flops | bytes accessed | tf_op | source)
XLA Modules:
  0.0 190.7 jit_solution(2314235694451149356)
XLA Ops:
  0.6 0.0 copy-start
  0.6 0.9 copy-done
  1.6 0.6 copy.10.match
  2.2 1.9 copy.15
  4.1 87.0 %shard_map.84 = (f32[32,4,48,512]{3,2,1,0:T(8,128)}, bf16[32,4,48,768]{3,2,1,0:T(8,128)(2,1)}, f32[32,8,256]{2,1,0:T(8,128)}, f32[32,8,256]{2,1,0:T(8,128)}, f32[8,256]{1,0:T(8,128)}) custom-call(bf16[256,768]{1,0:T(8,128)(2,1)} %q_ref.1, bf16[4,512,768]{2,1,0:T(8,128)(2,1)} %labels.3, bf16[4,1,768]{2,1,0:T(2,128)(2,1)} %copy.10.match, ...), custom_call_target="tpu_custom_call" | custom-call | tf_op jit(solution)/shard_map/pallas_call | solution.py:291
  91.1 1.3 slice.3
  92.3 41.0 %shard_map.85 = (bf16[32,256,768]{2,1,0:T(8,128)(2,1)}, bf16[4,512,768]{2,1,0:T(8,128)(2,1)}, f32[4,1,768]{2,1,0:T(1,128)}) custom-call(f32[32,4,48,512]{3,2,1,0:T(8,128)} %get-tuple-element.16.scores, bf16[32,4,48,768]{3,2,1,0:T(8,128)(2,1)} %get-tuple-element.17.rec, f32[32,8,256]{2,1,0:T(8,128)} %get-tuple-element.18.info, ...), custom_call_target="tpu_custom_call" | custom-call | tf_op jit(solution)/shard_map/pallas_call | solution.py:386
  133.4 51.8 %shard_map.86 = (f32[256,768]{1,0:T(8,128)}, f32[4,128,768]{2,1,0:T(8,128)}, f32[4,32,1,768]{3,2,1,0:T(1,128)}) custom-call(bf16[32,256,768]{2,1,0:T(8,128)(2,1)} %get-tuple-element.20.p, bf16[4,512,768]{2,1,0:T(8,128)(2,1)} %get-tuple-element.21.lp, f32[4,1,768]{2,1,0:T(1,128)} %get-tuple-element.22.ls), custom_call_target="tpu_custom_call" | custom-call | tf_op jit(solution)/shard_map/pallas_call | solution.py:551
  185.2 0.0 copy-start.1
  185.2 1.4 copy.12
  186.6 0.9 reshape.23
  187.4 2.1 %copy.18 = f32[256,768]{1,0:T(8,128)} copy(f32[256,768]{1,0:T(8,128)} %get-tuple-element.31) | data formatting | bytes 1572864
  189.5 0.0 copy-done.1
  189.5 1.1 copy.19
  (1 shorter events, 0.0 us)
Async XLA Ops:
  0.6 0.9 copy-start
  185.2 4.3 %copy-start.1 = (f32[4,128,768]{2,1,0:T(8,128)S(1)}, f32[4,128,768]{2,1,0:T(8,128)}, u32[]{:S(2)}) copy-start(f32[4,128,768]{2,1,0:T(8,128)} %get-tuple-element.32) | copy-start | bytes 4718596

commit v5 on v4

--- a/solution.py
+++ b/solution.py
@@ -65,6 +65,12 @@
 
 
 SLOTS = 48
+TURNS = (
+    ((0, 0), (1, 0), (2, 0), (0, 1)),
+    ((0, 2), (3, 0), (0, 3), (1, 1)),
+    ((1, 2), (2, 1), (2, 2), (1, 3)),
+    ((3, 1), (3, 2), (2, 3), (3, 3)),
+)
 
 
 def slot_tables(ids, pos):
@@ -117,6 +123,12 @@
         L.copy(q_ref, g.at[own], slot, to)
     g[own] = q_ref[...]
 
+    def tables(s, carry):
+        info[s] = slot_tables(ids_ref[s] - first, pos_ref[s])
+        return carry
+
+    lax.fori_loop(0, 32, tables, 0)
+
     def side_a(i):
         k = L.block(i, 0)
         L.wait(g.at[k], i - 1)
@@ -151,35 +163,43 @@
         L.wait(lo(k), 6 + 4 * i)
         L.wait(hi(k), 7 + 4 * i)
         L.copy(g.at[k], g.at[k], 23 + 4 * i, "p")
-        for j in range(4):
-            k = L.partner_block(i, j)
-            L.wait(g.at[k], 20 + 4 * i + j)
-
-    def work(i):
+
+    def work(turn, middle):
+        members = TURNS[turn]
+        for i, j in members:
+            L.wait(g.at[L.partner_block(i, j)], 20 + 4 * i + j)
+        code_a = sum(OFF[i] << (2 * n) for n, (i, j) in enumerate(members))
+        code_b = sum(OFF[j] << (2 * n) for n, (i, j) in enumerate(members))
+
         def block_of(n):
-            other, j = n // 4, lax.rem(n, 4)
+            other, m = n // 4, lax.rem(n, 4)
             core = L.core + other - 2 * L.core * other
-            a = lax.rem(L.a * (1 - other) + L.b * other + OFF[i], 4)
-            return index_of(core, a, j)
+            da = lax.rem(lax.shift_right_logical(jnp.int32(code_a), 2 * m), 4)
+            db = lax.rem(lax.shift_right_logical(jnp.int32(code_b), 2 * m), 4)
+            a = lax.rem(L.a * (1 - other) + L.b * other + da, 4)
+            b = lax.rem(L.b * (1 - other) + L.a * other + db, 4)
+            return index_of(core, a, b)
+
+        blocks = [L.block(i, j) for i, j in members] + [L.partner_block(i, j) for i, j in members]
 
         def pick(n, carry):
             s = block_of(n)
-            table = slot_tables(ids_ref[s] - first, pos_ref[s])
-            info[s] = table
+            table = info[s]
             one = jnp.concatenate([picks(table, c).astype(f32) for c in range(4)], axis=0)
             rows = jnp.dot(one.astype(jnp.bfloat16), g[s], preferred_element_type=f32)
             rec[s] = rows.astype(jnp.bfloat16).reshape(4, SLOTS, rows.shape[1])
             return carry
 
         lax.fori_loop(0, 8, pick, 0)
+        middle()
 
         def score(c, carry):
-            rows = jnp.concatenate([rec[block_of(n), c] for n in range(8)], axis=0)
+            rows = jnp.concatenate([rec[k, c] for k in blocks], axis=0)
             out = lax.dot_general(rows, labels[c], (((1,), (1,)), ((), ())), preferred_element_type=f32)
             bias = jnp.sum(rows.astype(f32) * match[c].astype(f32), axis=1, keepdims=True)
             out = out + bias
-            for n in range(8):
-                scores[block_of(n), c] = out[n * SLOTS : (n + 1) * SLOTS]
+            for n, k in enumerate(blocks):
+                scores[k, c] = out[n * SLOTS : (n + 1) * SLOTS]
             return carry
 
         lax.fori_loop(0, 4, score, 0)
@@ -213,34 +233,30 @@
             return carry
 
         lax.fori_loop(0, 8, stat, 0)
-        for core in range(2):
-            for j in range(4):
-                k = L.block(i, j) if core == 0 else L.partner_block(i, j)
-                n = 8 * i + 4 * core + j
-                pltpu.make_async_copy(scores.at[k], scores_out.at[k], out_sem.at[2 * n]).start()
-                pltpu.make_async_copy(rec.at[k], rec_out.at[k], out_sem.at[2 * n + 1]).start()
-                if n == 0:
-                    continue
-                pltpu.make_async_remote_copy(
-                    src_ref=st.at[k], dst_ref=sr.at[L.me], send_sem=st_send.at[k], recv_sem=st_recv.at[L.me],
-                    device_id={"label": k}, device_id_type=MESH,
-                ).start()
+        for m, k in enumerate(blocks):
+            n = 8 * turn + m
+            pltpu.make_async_copy(scores.at[k], scores_out.at[k], out_sem.at[2 * n]).start()
+            pltpu.make_async_copy(rec.at[k], rec_out.at[k], out_sem.at[2 * n + 1]).start()
+            if n == 0:
+                continue
+            pltpu.make_async_remote_copy(
+                src_ref=st.at[k], dst_ref=sr.at[L.me], send_sem=st_send.at[k], recv_sem=st_recv.at[L.me],
+                device_id={"label": k}, device_id_type=MESH,
+            ).start()
+        return blocks
 
     side_a(1)
     side_a(2)
     side_b(0)
-    far_a()
+    order = work(0, far_a)
     side_b(1)
     far_b(0)
-    work(0)
-    side_b(2)
+    order += work(1, lambda: side_b(2))
     far_b(1)
-    work(1)
-    side_b(3)
+    order += work(2, lambda: side_b(3))
     far_b(2)
-    work(2)
     far_b(3)
-    work(3)
+    order += work(3, lambda: None)
     sr[own] = st[own]
 
     def stat_copy(k, arrive):
@@ -256,7 +272,7 @@
     spread = jnp.sum(lines[:, 1:2, :] * jnp.exp(lines[:, 0:1, :] - best[None]), axis=0)
     chosen = jnp.sum(lines[:, 2:3, :], axis=0)
     value = best + jnp.log(spread)
-    losses[...] = jnp.broadcast_to(value - chosen, losses.shape)
+    losses[...] = value - chosen
     lse[own] = jnp.broadcast_to(value, lse.shape[1:])
 
     def lse_copy(dev, row):
@@ -272,13 +288,9 @@
     for k in peers:
         stat_copy(k, False).wait_send()
         lse_copy(k, own).wait_send()
-    for i in range(4):
-        for core in range(2):
-            for j in range(4):
-                k = L.block(i, j) if core == 0 else L.partner_block(i, j)
-                n = 8 * i + 4 * core + j
-                pltpu.make_async_copy(scores.at[k], scores_out.at[k], out_sem.at[2 * n]).wait()
-                pltpu.make_async_copy(rec.at[k], rec_out.at[k], out_sem.at[2 * n + 1]).wait()
+    for n, k in enumerate(order):
+        pltpu.make_async_copy(scores.at[k], scores_out.at[k], out_sem.at[2 * n]).wait()
+        pltpu.make_async_copy(rec.at[k], rec_out.at[k], out_sem.at[2 * n + 1]).wait()
     L.drain()
 
 
@@ -295,7 +307,7 @@
             shape((32, 4, SLOTS, width), bf16),
             shape((32, 8, q_dev), f32),
             shape((32, 8, q_dev), f32),
-            shape((8, q_dev), f32),
+            shape((1, q_dev), f32),
         ),
         in_specs=[vmem] * 5,
         out_specs=(hbm, hbm, vmem, vmem, vmem),
@@ -587,7 +599,7 @@
     partial, label_part, local_sum = backward(scores, received, info, lse, labels, match)
     query_grads, label_grads, rows = scatter(partial, label_part, local_sum)
     matcher_grads = rows.transpose(1, 0, 2, 3).reshape(matcher.shape)
-    return (losses[0], query_grads, label_grads, matcher_grads)
+    return (losses.reshape(q_dev), query_grads, label_grads, matcher_grads)
 
 
 def solution(mesh):

time: 192 us -> 177 us (0.922)
  Pallas kernels: 180 us -> 167 us
    pallas_call x1, Pallas kernels: 87 us -> 73.7 us  [forward(): pl.pallas_call(forward_kernel, out_shape=(shape((32, 4, SLOTS, LEAF), f32...]
    unnamed x6 -> x9, local copies, waits for them, and re-layouts: 4.13 us -> 4.7 us
where the time goes in v5:
time: 177 us
  Pallas kernels  167 us (94%)
  local copies, waits for them, and re-layouts  9.47 us (5%)
    pallas_call x1, Pallas kernels, forward(): pl.pallas_call(forward_kernel, out_shape=(shape((32, 4, SLOTS, LEAF), f32...  73.7 us
    pallas_call x1, Pallas kernels, scatter(): pl.pallas_call(scatter_kernel, out_shape=(shape((r, w), f32), shape((clus...  51.9 us
    pallas_call x1, Pallas kernels, backward(): pl.pallas_call(backward_kernel, grid=(n // group,), out_shape=(shape((n,...  41 us
    unnamed x9, local copies, waits for them, and re-layouts  4.7 us

profile of v5, /device:TPU:1, one launch (start us, length us, event | category | flops | bytes accessed | tf_op | source)
XLA Modules:
  0.0 176.8 jit_solution(5405449260513870567)
XLA Ops:
  0.6 0.0 copy-start
  0.6 0.9 copy-done
  1.6 0.6 copy.10.match
  2.2 1.9 %copy.15 = s32[2,32,8,256]{3,2,0,1:T(8,128)} copy(s32[2,32,8,256]{3,2,1,0:T(8,128)} %bitcast.15) | data formatting | bytes 1048576 | tf_op jit(solution)/shard_map/reshape | solution.py:596
  4.1 73.7 %shard_map.84 = (f32[32,4,48,512]{3,2,1,0:T(8,128)}, bf16[32,4,48,768]{3,2,1,0:T(8,128)(2,1)}, f32[32,8,256]{2,1,0:T(8,128)}, f32[32,8,256]{2,1,0:T(8,128)}, f32[1,256]{1,0:T(1,128)}) custom-call(bf16[256,768]{1,0:T(8,128)(2,1)} %q_ref.1, bf16[4,512,768]{2,1,0:T(8,128)(2,1)} %labels.3, bf16[4,1,768]{2,1,0:T(2,128)(2,1)} %copy.10.match, ...), custom_call_target="tpu_custom_call" | custom-call | tf_op jit(solution)/shard_map/pallas_call | solution.py:303
  77.8 41.0 %shard_map.85 = (bf16[32,256,768]{2,1,0:T(8,128)(2,1)}, bf16[4,512,768]{2,1,0:T(8,128)(2,1)}, f32[4,1,768]{2,1,0:T(1,128)}) custom-call(f32[32,4,48,512]{3,2,1,0:T(8,128)} %get-tuple-element.16.scores, bf16[32,4,48,768]{3,2,1,0:T(8,128)(2,1)} %get-tuple-element.17.rec, f32[32,8,256]{2,1,0:T(8,128)} %get-tuple-element.18.info, ...), custom_call_target="tpu_custom_call" | custom-call | tf_op jit(solution)/shard_map/pallas_call | solution.py:398
  118.9 0.0 copy-start.2
  118.9 51.9 %shard_map.86 = (f32[256,768]{1,0:T(8,128)}, f32[4,128,768]{2,1,0:T(8,128)}, f32[4,32,1,768]{3,2,1,0:T(1,128)}) custom-call(bf16[32,256,768]{2,1,0:T(8,128)(2,1)} %get-tuple-element.20.p, bf16[4,512,768]{2,1,0:T(8,128)(2,1)} %get-tuple-element.21.lp, f32[4,1,768]{2,1,0:T(1,128)} %get-tuple-element.22.ls), custom_call_target="tpu_custom_call" | custom-call | tf_op jit(solution)/shard_map/pallas_call | solution.py:563
  170.8 0.0 copy-start.1
  170.8 1.4 copy.12
  172.2 0.9 reshape.27
  173.1 0.0 copy-done.2
  173.1 0.6 copy.19
  173.6 2.1 %copy.20 = f32[256,768]{1,0:T(8,128)} copy(f32[256,768]{1,0:T(8,128)} %get-tuple-element.31) | data formatting | bytes 1572864
  175.7 0.0 copy-done.1
  175.7 1.1 copy.21
  (1 shorter events, 0.0 us)
Async XLA Ops:
  0.6 0.9 copy-start
  118.9 54.2 %copy-start.2 = (f32[1,256]{1,0:T(1,128)S(1)}, f32[1,256]{1,0:T(1,128)}, u32[]{:S(2)}) copy-start(f32[1,256]{1,0:T(1,128)} %get-tuple-element.15) | copy-start | bytes 3076
  170.8 4.9 %copy-start.1 = (f32[4,128,768]{2,1,0:T(8,128)S(1)}, f32[4,128,768]{2,1,0:T(8,128)}, u32[]{:S(2)}) copy-start(f32[4,128,768]{2,1,0:T(8,128)} %get-tuple-element.32) | copy-start | bytes 4718596

commit v6 on v5

--- a/solution.py
+++ b/solution.py
@@ -325,107 +325,6 @@
     )(q, labels, match, ids, pos)
 
 
-def backward_kernel(scores, rec, info, lse, labels, match, partial, label_part, local_sum,
-                    delta, coef, grads, held):
-    f32, bf16 = jnp.float32, jnp.bfloat16
-    step = pl.program_id(0)
-    blocks = scores.shape[0]
-
-    @pl.when(step == 0)
-    def _():
-        local_sum[...] = jnp.zeros_like(local_sum)
-
-    def part(n, carry):
-        table = info[n]
-        leaf = lax.broadcasted_iota(jnp.int32, (SLOTS, LEAF), 1).astype(f32)
-        log_sum = lse[n, 0:1]
-        for c in range(4):
-            one = picks(table, c)
-            used = jnp.sum(jnp.where(one, 1.0, 0.0), axis=1, keepdims=True) > 0.5
-            norm = jnp.sum(jnp.where(one, log_sum, 0.0), axis=1, keepdims=True)
-            norm = jnp.where(used, norm, BIG)
-            hit = leaf == target_column(table, one, c)
-            value = jnp.exp(scores[n, c] - norm) - hit.astype(f32)
-            total = jnp.sum(value, axis=1, keepdims=True).astype(bf16)
-            rows = pl.ds(pl.multiple_of((step * blocks + n) * SLOTS, 16), SLOTS)
-            delta[c, rows] = value.astype(bf16)
-            coef[c, pl.ds(pl.multiple_of(n * SLOTS, 16), SLOTS)] = jnp.broadcast_to(total.astype(f32), (SLOTS, 128))
-            local_sum[c] += jnp.sum(total.astype(f32) * rec[n, c].astype(f32), axis=0, keepdims=True)
-        return carry
-
-    lax.fori_loop(0, blocks, part, 0)
-
-    def slot(c, carry):
-        rows = pl.ds(pl.multiple_of(step * blocks * SLOTS, 16), blocks * SLOTS)
-        out = jnp.dot(delta[c, rows], labels[c], preferred_element_type=f32)
-        out = out + coef[c][:, 0:1] * match[c].astype(f32)
-        out = out.astype(bf16)
-        for n in range(blocks):
-            grads[n, pl.ds(pl.multiple_of(c * SLOTS, 16), SLOTS)] = out[n * SLOTS : (n + 1) * SLOTS]
-        return carry
-
-    lax.fori_loop(0, 4, slot, 0)
-
-    def back(n, carry):
-        table = info[n]
-        one = jnp.concatenate([picks(table, c).astype(f32) for c in range(4)], axis=0).astype(bf16)
-        out = lax.dot_general(one, grads[n], (((0,), (0,)), ((), ())), preferred_element_type=f32)
-        partial[n] = out.astype(bf16)
-        return carry
-
-    lax.fori_loop(0, blocks, back, 0)
-
-    for n in range(blocks):
-        held[:, pl.ds(pl.multiple_of((step * blocks + n) * SLOTS, 16), SLOTS)] = rec[n]
-
-    @pl.when(step == pl.num_programs(0) - 1)
-    def _():
-        def gather_part(c, carry):
-            out = lax.dot_general(delta[c], held[c], (((0,), (0,)), ((), ())), preferred_element_type=f32)
-            label_part[c] = out.astype(bf16)
-            return carry
-
-        lax.fori_loop(0, 4, gather_part, 0)
-
-
-def backward(scores, rec, info, lse, labels, match):
-    n, _, _, width = rec.shape
-    q_dev = info.shape[2]
-    f32, bf16 = jnp.float32, jnp.bfloat16
-    group = 8
-    vmem = pl.BlockSpec(memory_space=pltpu.VMEM)
-    shape = jax.ShapeDtypeStruct
-    return pl.pallas_call(
-        backward_kernel,
-        grid=(n // group,),
-        out_shape=(
-            shape((n, q_dev, width), bf16),
-            shape((4, LEAF, width), bf16),
-            shape((4, 1, width), f32),
-        ),
-        in_specs=[
-            pl.BlockSpec((group, 4, SLOTS, LEAF), lambda i: (i, 0, 0, 0)),
-            pl.BlockSpec((group, 4, SLOTS, width), lambda i: (i, 0, 0, 0)),
-            pl.BlockSpec((group, 8, q_dev), lambda i: (i, 0, 0)),
-            pl.BlockSpec((group, 8, q_dev), lambda i: (i, 0, 0)),
-            vmem,
-            vmem,
-        ],
-        out_specs=(
-            pl.BlockSpec((group, q_dev, width), lambda i: (i, 0, 0)),
-            vmem,
-            vmem,
-        ),
-        scratch_shapes=[
-            pltpu.VMEM((4, n * SLOTS, LEAF), bf16),
-            pltpu.VMEM((4, group * SLOTS, 128), f32),
-            pltpu.VMEM((group, 4 * SLOTS, width), bf16),
-            pltpu.VMEM((4, n * SLOTS, width), bf16),
-        ],
-        compiler_params=pltpu.CompilerParams(vmem_limit_bytes=60 * 1024 * 1024),
-    )(scores, rec, info, lse, labels, match)
-
-
 class Column:
     def __init__(self, links):
         self.z = lax.axis_index("dp")
@@ -442,10 +341,43 @@
         L.sent.append(c)
 
 
-def scatter_kernel(p, lp, ls, out, label_out, mout, t_all, u, pr, bh, bf, ah, af, zt, zh, zf, mz, send, recv, m_recv):
+BACK_TURNS = (
+    ((3, 3), (1, 3), (2, 3), (0, 3)),
+    ((3, 1), (3, 2), (1, 1), (1, 2)),
+    ((2, 1), (2, 2), (0, 1), (0, 2)),
+    ((3, 0), (1, 0), (2, 0), (0, 0)),
+)
+
+
+def backward_kernel(labels, match, info, lse, scores_hbm, rec_hbm, out, label_out, mout,
+                    stage, rec, delta, coef, grads, p, lp, ls, pr, bh, bf, ah, af, zt, zh, zf, mz,
+                    send, recv, m_recv, in_sem):
     L = Links(send, recv)
     Z = Column(L)
     z = Z.z
+    f32, bf16 = jnp.float32, jnp.bfloat16
+    turns = [
+        [L.block(i, j) for i, j in t] + [L.partner_block(i, j) for i, j in t] for t in BACK_TURNS
+    ]
+
+    def load_scores(t):
+        return [
+            pltpu.make_async_copy(scores_hbm.at[k], stage.at[t % 2, m], in_sem.at[0, 8 * t + m])
+            for m, k in enumerate(turns[t])
+        ]
+
+    def load_rows(t):
+        return [
+            pltpu.make_async_copy(rec_hbm.at[k], rec.at[k], in_sem.at[1, 8 * t + m])
+            for m, k in enumerate(turns[t])
+        ]
+
+    for t in range(2):
+        for c in load_scores(t) + load_rows(t):
+            c.start()
+    for t in range(2, 4):
+        for c in load_rows(t):
+            c.start()
     peers = [L.block(i, j) for i in range(4) for j in range(4)][1:]
     peers += [L.partner_block(i, j) for i in range(4) for j in range(4)]
     barrier = pltpu.get_barrier_semaphore()
@@ -453,38 +385,119 @@
         pl.semaphore_signal(barrier, inc=1, device_id={"label": d}, device_id_type=MESH)
     for off in (1, 2, 3):
         pl.semaphore_signal(barrier, inc=1, device_id={"dp": lax.rem(z + off, 4)}, device_id_type=MESH)
-    pl.semaphore_wait(barrier, 34)
+    ls[...] = jnp.zeros_like(ls)
+
+    def block_of(t, n):
+        code_a = sum(OFF[i] << (2 * m) for m, (i, j) in enumerate(BACK_TURNS[t]))
+        code_b = sum(OFF[j] << (2 * m) for m, (i, j) in enumerate(BACK_TURNS[t]))
+        other, m = n // 4, lax.rem(n, 4)
+        core = L.core + other - 2 * L.core * other
+        da = lax.rem(lax.shift_right_logical(jnp.int32(code_a), 2 * m), 4)
+        db = lax.rem(lax.shift_right_logical(jnp.int32(code_b), 2 * m), 4)
+        a = lax.rem(L.a * (1 - other) + L.b * other + da, 4)
+        b = lax.rem(L.b * (1 - other) + L.a * other + db, 4)
+        return index_of(core, a, b)
+
+    def part(t):
+        for c in load_scores(t) + load_rows(t):
+            c.wait()
+
+        def step(n, carry):
+            k = block_of(t, n)
+            table = info[k]
+            leaf = lax.broadcasted_iota(jnp.int32, (SLOTS, LEAF), 1).astype(f32)
+            log_sum = lse[k, 0:1]
+            for c in range(4):
+                one = picks(table, c)
+                used = jnp.sum(jnp.where(one, 1.0, 0.0), axis=1, keepdims=True) > 0.5
+                norm = jnp.sum(jnp.where(one, log_sum, 0.0), axis=1, keepdims=True)
+                norm = jnp.where(used, norm, BIG)
+                hit = leaf == target_column(table, one, c)
+                value = jnp.exp(stage[t % 2, n, c] - norm) - hit.astype(f32)
+                total = jnp.sum(value, axis=1, keepdims=True).astype(bf16)
+                delta[k, c] = value.astype(bf16)
+                coef[k, c] = jnp.broadcast_to(total.astype(f32), (SLOTS, 128)).astype(bf16)
+                ls[c] += jnp.sum(total.astype(f32) * rec[k, c].astype(f32), axis=0, keepdims=True)
+            return carry
+
+        lax.fori_loop(0, 8, step, 0)
+        if t < 2:
+            for c in load_scores(t + 2):
+                c.start()
+
+    def slots(t):
+        def slot(c, carry):
+            rows = jnp.concatenate([delta[k, c] for k in turns[t]], axis=0)
+            scale = jnp.concatenate([coef[k, c] for k in turns[t]], axis=0)[:, 0:1].astype(f32)
+            val = jnp.dot(rows, labels[c], preferred_element_type=f32)
+            val = (val + scale * match[c].astype(f32)).astype(bf16)
+            for n in range(8):
+                grads[n, pl.ds(pl.multiple_of(c * SLOTS, 16), SLOTS)] = val[n * SLOTS : (n + 1) * SLOTS]
+            return carry
+
+        lax.fori_loop(0, 4, slot, 0)
+
+        def back(n, carry):
+            k = block_of(t, n)
+            table = info[k]
+            one = jnp.concatenate([picks(table, c).astype(f32) for c in range(4)], axis=0).astype(bf16)
+            val = lax.dot_general(one, grads[n], (((0,), (0,)), ((), ())), preferred_element_type=f32)
+            p[k] = val.astype(bf16)
+            return carry
+
+        lax.fori_loop(0, 8, back, 0)
+        for i, j in BACK_TURNS[t]:
+            L.copy(p.at[L.partner_block(i, j)], pr.at[4 * i + j], 4 * i + j, "p")
+
+    def label_parts(low):
+        def one_part(c, carry):
+            left = jnp.concatenate([delta[k, c] for k in range(32)], axis=0)
+            right = jnp.concatenate([rec[k, c] for k in range(32)], axis=0)
+            val = lax.dot_general(left, right, (((0,), (0,)), ((), ())), preferred_element_type=f32)
+            lp[c] = val.astype(bf16)
+            return carry
+
+        lax.fori_loop(low, low + 2, one_part, 0)
+
     half = p.shape[1] // 2
-    f32 = jnp.float32
     rows_z = label_out.shape[1]
 
     def rows(off):
         return pl.ds(pl.multiple_of(lax.rem(z + off, 4) * rows_z, rows_z), rows_z)
 
     PAIRS = pl.ds(0, 2), pl.ds(2, 2)
-    for off in (1, 2, 3):
-        Z.copy(ls.at[lax.rem(z + off, 4)], mz.at[z], 41 + off, off)
-    ORDER = [(i, 3) for i in (3, 1, 2, 0)] + [(i, j) for i in (3, 1, 2, 0) for j in (1, 2)] + [(i, 0) for i in (3, 1, 2, 0)]
-    for i, j in ORDER:
-        L.copy(p.at[L.partner_block(i, j)], pr.at[4 * i + j], 4 * i + j, "p")
-    Z.copy(lp.at[PAIRS[0], rows(2)], zh.at[0], 36, 1)
-    Z.copy(lp.at[PAIRS[1], rows(2)], zh.at[1], 37, 3)
     LO, HI = pl.ds(0, half), pl.ds(half, half)
-    mz[z] = ls[z]
 
     def both(i, j):
         L.wait(pr.at[4 * i + j], 4 * i + j)
         return lambda s: p[L.block(i, j), s].astype(f32) + pr[4 * i + j, s].astype(f32)
 
-    for i in (3, 1, 2, 0):
+    def far(i):
         s = both(i, 3)
-        t = t_all.at[3 * i + 2]
+        t = p.at[L.block(i, 3)]
         t[...] = s(slice(None)).astype(t.dtype)
         L.copy(t.at[LO], bh.at[i, 0], 16 + 4 * i, "b+")
         L.copy(t.at[HI], bh.at[i, 1], 17 + 4 * i, "b-")
-    for off in (1, 2, 3):
-        L.wait(mz.at[lax.rem(z + 4 - off, 4)], 41 + off)
-    mout[z, L.me] = mz[0] + mz[1] + mz[2] + mz[3]
+
+    def near(i):
+        s = both(i, 2)
+        t = p.at[L.block(i, 2)]
+        L.wait(bh.at[i, 0], 16 + 4 * i)
+        t[LO] = (s(LO) + bh[i, 0].astype(f32)).astype(t.dtype)
+        t[HI] = s(HI).astype(t.dtype)
+        L.copy(t, bf.at[i, 0], 18 + 4 * i, "b+")
+        s = both(i, 1)
+        t = p.at[L.block(i, 1)]
+        L.wait(bh.at[i, 1], 17 + 4 * i)
+        t[HI] = (s(HI) + bh[i, 1].astype(f32)).astype(t.dtype)
+        t[LO] = s(LO).astype(t.dtype)
+        L.copy(t, bf.at[i, 1], 19 + 4 * i, "b-")
+
+    def column(i):
+        s = both(i, 0)
+        L.wait(bf.at[i, 0], 18 + 4 * i)
+        L.wait(bf.at[i, 1], 19 + 4 * i)
+        return lambda r: s(r) + bf[i, 0, r].astype(f32) + bf[i, 1, r].astype(f32)
 
     def row_copy(dev, row):
         return pltpu.make_async_remote_copy(
@@ -492,54 +505,62 @@
             device_id={"label": dev}, device_id_type=MESH,
         )
 
+    part(0)
+    pl.semaphore_wait(barrier, 34)
+    slots(0)
+    part(1)
+    for i in (3, 1, 2, 0):
+        far(i)
+    part(2)
+    part(3)
+    mz[z] = ls[z]
+    for off in (1, 2, 3):
+        Z.copy(ls.at[lax.rem(z + off, 4)], mz.at[z], 41 + off, off)
+    slots(1)
+    label_parts(0)
+    Z.copy(lp.at[PAIRS[0], rows(2)], zh.at[0], 36, 1)
+    near(3)
+    near(1)
+    label_parts(2)
+    Z.copy(lp.at[PAIRS[1], rows(2)], zh.at[1], 37, 3)
+    for off in (1, 2, 3):
+        L.wait(mz.at[lax.rem(z + 4 - off, 4)], 41 + off)
+    mout[z, L.me] = mz[0] + mz[1] + mz[2] + mz[3]
     for k in peers:
         row_copy(k, L.me).start()
+    slots(2)
     L.wait(zh.at[0], 36)
     zt[1, 0:2] = (lp[PAIRS[0], rows(1)].astype(f32) + zh[0].astype(f32)).astype(zt.dtype)
     zt[1, 2:4] = lp[PAIRS[1], rows(1)]
     Z.copy(zt.at[1], zf.at[0], 38, 1)
+    near(2)
+    near(0)
     L.wait(zh.at[1], 37)
     zt[0, 2:4] = (lp[PAIRS[1], rows(3)].astype(f32) + zh[1].astype(f32)).astype(zt.dtype)
     zt[0, 0:2] = lp[PAIRS[0], rows(3)]
     Z.copy(zt.at[0], zf.at[1], 39, 3)
-    for i in (3, 1, 2, 0):
-        s = both(i, 2)
-        t = t_all.at[3 * i + 1]
-        L.wait(bh.at[i, 0], 16 + 4 * i)
-        t[LO] = (s(LO) + bh[i, 0].astype(f32)).astype(t.dtype)
-        t[HI] = s(HI).astype(t.dtype)
-        L.copy(t, bf.at[i, 0], 18 + 4 * i, "b+")
-        s = both(i, 1)
-        t = t_all.at[3 * i + 0]
-        L.wait(bh.at[i, 1], 17 + 4 * i)
-        t[HI] = (s(HI) + bh[i, 1].astype(f32)).astype(t.dtype)
-        t[LO] = s(LO).astype(t.dtype)
-        L.copy(t, bf.at[i, 1], 19 + 4 * i, "b-")
+    slots(3)
     for k in peers:
         row_copy(k, k).wait_recv()
     for off in (1, 2, 3):
         Z.copy(mout.at[z], mout.at[z], 44 + off, off)
-
-    def column(i):
-        s = both(i, 0)
-        L.wait(bf.at[i, 0], 18 + 4 * i)
-        L.wait(bf.at[i, 1], 19 + 4 * i)
-        return lambda r: s(r) + bf[i, 0, r].astype(f32) + bf[i, 1, r].astype(f32)
-
     s = column(3)
-    u[2] = s(slice(None)).astype(u.dtype)
-    L.copy(u.at[2, LO], ah.at[0], 32, "a+")
-    L.copy(u.at[2, HI], ah.at[1], 33, "a-")
+    u = p.at[L.block(3, 0)]
+    u[...] = s(slice(None)).astype(u.dtype)
+    L.copy(u.at[LO], ah.at[0], 32, "a+")
+    L.copy(u.at[HI], ah.at[1], 33, "a-")
     s = column(1)
+    u = p.at[L.block(1, 0)]
     L.wait(ah.at[1], 33)
-    u[0, HI] = (s(HI) + ah[1].astype(f32)).astype(u.dtype)
-    u[0, LO] = s(LO).astype(u.dtype)
-    L.copy(u.at[0], af.at[1], 35, "a-")
+    u[HI] = (s(HI) + ah[1].astype(f32)).astype(u.dtype)
+    u[LO] = s(LO).astype(u.dtype)
+    L.copy(u, af.at[1], 35, "a-")
     s = column(2)
+    u = p.at[L.block(2, 0)]
     L.wait(ah.at[0], 32)
-    u[1, LO] = (s(LO) + ah[0].astype(f32)).astype(u.dtype)
-    u[1, HI] = s(HI).astype(u.dtype)
-    L.copy(u.at[1], af.at[0], 34, "a+")
+    u[LO] = (s(LO) + ah[0].astype(f32)).astype(u.dtype)
+    u[HI] = s(HI).astype(u.dtype)
+    L.copy(u, af.at[0], 34, "a+")
     L.wait(zf.at[0], 38)
     L.wait(zf.at[1], 39)
     label_out[...] = lp[:, rows(0)].astype(f32) + zf[0].astype(f32) + zf[1].astype(f32)
@@ -554,20 +575,27 @@
     L.drain()
 
 
-def scatter(p, lp, ls):
-    n, r, w = p.shape
-    clusters, leaf, _ = lp.shape
+def backward(labels, match, info, lse, scores, rec):
+    n, _, r = info.shape
+    clusters, leaf, w = labels.shape
     f32, bf16, dma = jnp.float32, jnp.bfloat16, pltpu.SemaphoreType.DMA
     vmem = pl.BlockSpec(memory_space=pltpu.VMEM)
+    hbm = pl.BlockSpec(memory_space=pl.ANY)
     shape = jax.ShapeDtypeStruct
     return pl.pallas_call(
-        scatter_kernel,
+        backward_kernel,
         out_shape=(shape((r, w), f32), shape((clusters, leaf // 4, w), f32), shape((4, n, 1, w), f32)),
-        in_specs=[vmem] * 3,
+        in_specs=[vmem] * 4 + [hbm] * 2,
         out_specs=(vmem,) * 3,
         scratch_shapes=[
-            pltpu.VMEM((12, r, w), bf16),
-            pltpu.VMEM((3, r, w), bf16),
+            pltpu.VMEM((2, 8, 4, SLOTS, leaf), f32),
+            pltpu.VMEM((n, 4, SLOTS, w), bf16),
+            pltpu.VMEM((n, 4, SLOTS, leaf), bf16),
+            pltpu.VMEM((n, 4, SLOTS, 128), bf16),
+            pltpu.VMEM((8, 4 * SLOTS, w), bf16),
+            pltpu.VMEM((n, r, w), bf16),
+            pltpu.VMEM((clusters, leaf, w), bf16),
+            pltpu.VMEM((clusters, 1, w), f32),
             pltpu.VMEM((16, r, w), bf16),
             pltpu.VMEM((4, 2, r // 2, w), bf16),
             pltpu.VMEM((4, 2, r, w), bf16),
@@ -580,11 +608,12 @@
             dma((52,)),
             dma((48,)),
             dma((2, 32)),
+            dma((2, 32)),
         ],
         compiler_params=pltpu.CompilerParams(
-            collective_id=1, has_side_effects=True, vmem_limit_bytes=60 * 1024 * 1024
+            collective_id=1, has_side_effects=True, vmem_limit_bytes=67043328
         ),
-    )(p, lp, ls)
+    )(labels, match, info, lse, scores, rec)
 
 
 def body(queries, labels, matcher, cluster_ids, positives):
@@ -596,8 +625,7 @@
     ids = cluster_ids.reshape(n_label, q_dev, K).transpose(0, 2, 1)
     pos = positives.reshape(n_label, 1, q_dev)
     scores, received, info, lse, losses = forward(queries, labels, match, ids, pos)
-    partial, label_part, local_sum = backward(scores, received, info, lse, labels, match)
-    query_grads, label_grads, rows = scatter(partial, label_part, local_sum)
+    query_grads, label_grads, rows = backward(labels, match, info, lse, scores, received)
     matcher_grads = rows.transpose(1, 0, 2, 3).reshape(matcher.shape)
     return (losses.reshape(q_dev), query_grads, label_grads, matcher_grads)
 

time: 177 us -> 153 us (0.86)
  Pallas kernels: 167 us -> 142 us
    pallas_call x2 -> x1, Pallas kernels: 92.9 us -> 68.5 us  [backward(): pl.pallas_call(backward_kernel, out_shape=(shape((r, w), f32), shape((clu...]
    unnamed x9 -> x5, local copies, waits for them, and re-layouts: 4.7 us -> 4.44 us
where the time goes in v6:
time: 153 us
  Pallas kernels  142 us (93%)
  local copies, waits for them, and re-layouts  9.92 us (6%)
    pallas_call x1, Pallas kernels, forward(): pl.pallas_call(forward_kernel, out_shape=(shape((32, 4, SLOTS, LEAF), f32...  73.8 us
    pallas_call x1, Pallas kernels, backward(): pl.pallas_call(backward_kernel, out_shape=(shape((r, w), f32), shape((clu...  68.5 us
    unnamed x5, local copies, waits for them, and re-layouts  4.44 us

profile of v6, /device:TPU:1, one launch (start us, length us, event | category | flops | bytes accessed | tf_op | source)
XLA Modules:
  0.0 152.9 jit_solution(7455525306727663495)
XLA Ops:
  0.6 0.7 dynamic-slice_bitcast_fusion
  1.4 0.6 copy.10.match
  2.0 1.9 %copy.15 = s32[2,32,8,256]{3,2,0,1:T(8,128)} copy(s32[2,32,8,256]{3,2,1,0:T(8,128)} %bitcast.15) | data formatting | bytes 1048576 | tf_op jit(solution)/shard_map/reshape | solution.py:625
  3.9 73.8 %shard_map.84 = (f32[32,4,48,512]{3,2,1,0:T(8,128)}, bf16[32,4,48,768]{3,2,1,0:T(8,128)(2,1)}, f32[32,8,256]{2,1,0:T(8,128)}, f32[32,8,256]{2,1,0:T(8,128)}, f32[1,256]{1,0:T(1,128)}) custom-call(bf16[256,768]{1,0:T(8,128)(2,1)} %q_ref.1, bf16[4,512,768]{2,1,0:T(8,128)(2,1)} %labels.3, bf16[4,1,768]{2,1,0:T(2,128)(2,1)} %copy.10.match, ...), custom_call_target="tpu_custom_call" | custom-call | tf_op jit(solution)/shard_map/pallas_call | solution.py:303
  77.7 68.5 %shard_map.85 = (f32[256,768]{1,0:T(8,128)}, f32[4,128,768]{2,1,0:T(8,128)}, f32[4,32,1,768]{3,2,1,0:T(1,128)}) custom-call(bf16[4,512,768]{2,1,0:T(8,128)(2,1)} %labels.3, bf16[4,1,768]{2,1,0:T(2,128)(2,1)} %copy.10.match, f32[32,8,256]{2,1,0:T(8,128)} %get-tuple-element.13.info, f32[32,8,256]{2,1,0:T(8,128)} %get-tuple-element.14.lse, ...), custom_call_target="tpu_custom_call" | custom-call | tf_op jit(solution)/shard_map/pallas_call | solution.py:585
  146.2 0.0 copy-start
  146.2 1.4 copy.12
  147.6 0.9 reshape.27
  148.5 1.2 copy.19
  149.7 2.1 %copy.20 = f32[256,768]{1,0:T(8,128)} copy(f32[256,768]{1,0:T(8,128)} %get-tuple-element.25) | data formatting | bytes 1572864
  151.8 0.0 copy-done
  151.8 1.1 copy.21
Async XLA Ops:
  146.2 5.6 %copy-start = (f32[4,128,768]{2,1,0:T(8,128)S(1)}, f32[4,128,768]{2,1,0:T(8,128)}, u32[]{:S(2)}) copy-start(f32[4,128,768]{2,1,0:T(8,128)} %get-tuple-element.26) | copy-start | bytes 4718596

commit v7 on v6

--- a/solution.py
+++ b/solution.py
@@ -66,10 +66,10 @@
 
 SLOTS = 48
 TURNS = (
-    ((0, 0), (1, 0), (2, 0), (0, 1)),
-    ((0, 2), (3, 0), (0, 3), (1, 1)),
-    ((1, 2), (2, 1), (2, 2), (1, 3)),
-    ((3, 1), (3, 2), (2, 3), (3, 3)),
+    ((0, 0), (1, 0), (2, 0), (0, 1), (0, 2)),
+    ((3, 0), (0, 3), (1, 1), (1, 2)),
+    ((2, 1), (2, 2), (1, 3), (3, 1), (3, 2)),
+    ((2, 3), (3, 3)),
 )
 
 
@@ -166,13 +166,15 @@
 
     def work(turn, middle):
         members = TURNS[turn]
+        size = len(members)
+        base = 2 * sum(len(t) for t in TURNS[:turn])
         for i, j in members:
             L.wait(g.at[L.partner_block(i, j)], 20 + 4 * i + j)
         code_a = sum(OFF[i] << (2 * n) for n, (i, j) in enumerate(members))
         code_b = sum(OFF[j] << (2 * n) for n, (i, j) in enumerate(members))
 
         def block_of(n):
-            other, m = n // 4, lax.rem(n, 4)
+            other, m = n // size, lax.rem(n, size)
             core = L.core + other - 2 * L.core * other
             da = lax.rem(lax.shift_right_logical(jnp.int32(code_a), 2 * m), 4)
             db = lax.rem(lax.shift_right_logical(jnp.int32(code_b), 2 * m), 4)
@@ -190,7 +192,7 @@
             rec[s] = rows.astype(jnp.bfloat16).reshape(4, SLOTS, rows.shape[1])
             return carry
 
-        lax.fori_loop(0, 8, pick, 0)
+        lax.fori_loop(0, 2 * size, pick, 0)
         middle()
 
         def score(c, carry):
@@ -228,13 +230,12 @@
                     jnp.where(one, total * jnp.exp(jnp.where(one, top - best, 0.0)), 0.0), axis=0, keepdims=True
                 )
                 chosen += jnp.sum(jnp.where(one, picked, 0.0), axis=0, keepdims=True)
-            line = lax.broadcasted_iota(jnp.int32, (8, table.shape[1]), 0)
-            st[s] = jnp.where(line == 0, best, jnp.where(line == 1, spread, chosen))
+            st[s] = jnp.concatenate([best, spread, chosen], axis=1)
             return carry
 
-        lax.fori_loop(0, 8, stat, 0)
+        lax.fori_loop(0, 2 * size, stat, 0)
         for m, k in enumerate(blocks):
-            n = 8 * turn + m
+            n = base + m
             pltpu.make_async_copy(scores.at[k], scores_out.at[k], out_sem.at[2 * n]).start()
             pltpu.make_async_copy(rec.at[k], rec_out.at[k], out_sem.at[2 * n + 1]).start()
             if n == 0:
@@ -249,12 +250,12 @@
     side_a(2)
     side_b(0)
     order = work(0, far_a)
+    far_b(0)
     side_b(1)
-    far_b(0)
     order += work(1, lambda: side_b(2))
     far_b(1)
-    order += work(2, lambda: side_b(3))
-    far_b(2)
+    side_b(3)
+    order += work(2, lambda: far_b(2))
     far_b(3)
     order += work(3, lambda: None)
     sr[own] = st[own]
@@ -267,13 +268,14 @@
 
     for k in peers:
         stat_copy(k, True).wait_recv()
-    best = jnp.max(sr[:, 0:1, :], axis=0)
-    lines = sr[...]
-    spread = jnp.sum(lines[:, 1:2, :] * jnp.exp(lines[:, 0:1, :] - best[None]), axis=0)
-    chosen = jnp.sum(lines[:, 2:3, :], axis=0)
+    q_dev = q_ref.shape[0]
+    tops = sr[:, :, 0:q_dev]
+    best = jnp.max(tops, axis=0)
+    spread = jnp.sum(sr[:, :, q_dev : 2 * q_dev] * jnp.exp(tops - best[None]), axis=0)
+    chosen = jnp.sum(sr[:, :, 2 * q_dev : 3 * q_dev], axis=0)
     value = best + jnp.log(spread)
     losses[...] = value - chosen
-    lse[own] = jnp.broadcast_to(value, lse.shape[1:])
+    lse[own] = value
 
     def lse_copy(dev, row):
         return pltpu.make_async_remote_copy(
@@ -306,7 +308,7 @@
             shape((32, 4, SLOTS, LEAF), f32),
             shape((32, 4, SLOTS, width), bf16),
             shape((32, 8, q_dev), f32),
-            shape((32, 8, q_dev), f32),
+            shape((32, 1, q_dev), f32),
             shape((1, q_dev), f32),
         ),
         in_specs=[vmem] * 5,
@@ -315,8 +317,8 @@
             pltpu.VMEM((32, q_dev, width), bf16),
             pltpu.VMEM((32, 4, SLOTS, LEAF), f32),
             pltpu.VMEM((32, 4, SLOTS, width), bf16),
-            pltpu.VMEM((32, 8, q_dev), f32),
-            pltpu.VMEM((32, 8, q_dev), f32),
+            pltpu.VMEM((32, 1, 3 * q_dev), f32),
+            pltpu.VMEM((32, 1, 3 * q_dev), f32),
             dma((36,)), dma((36,)), dma((32,)), dma((32,)), dma((32,)), dma((32,)), dma((64,)),
         ],
         compiler_params=pltpu.CompilerParams(
@@ -342,15 +344,15 @@
 
 
 BACK_TURNS = (
-    ((3, 3), (1, 3), (2, 3), (0, 3)),
-    ((3, 1), (3, 2), (1, 1), (1, 2)),
-    ((2, 1), (2, 2), (0, 1), (0, 2)),
-    ((3, 0), (1, 0), (2, 0), (0, 0)),
+    ((3, 3), (3, 1), (3, 2), (1, 3)),
+    ((2, 3), (3, 0), (1, 1), (1, 2)),
+    ((2, 1), (2, 2), (0, 3), (1, 0)),
+    ((2, 0), (0, 1), (0, 2), (0, 0)),
 )
 
 
-def backward_kernel(labels, match, info, lse, scores_hbm, rec_hbm, out, label_out, mout,
-                    stage, rec, delta, coef, grads, p, lp, ls, pr, bh, bf, ah, af, zt, zh, zf, mz,
+def backward_kernel(labels, match, info, lse, scores_hbm, rec_hbm, out, label_out, matcher_out,
+                    mout, stage, rec, delta, coef, grads, p, lp, ls, pr, bh, bf, ah, af, zh, zf, mz,
                     send, recv, m_recv, in_sem):
     L = Links(send, recv)
     Z = Column(L)
@@ -406,7 +408,7 @@
             k = block_of(t, n)
             table = info[k]
             leaf = lax.broadcasted_iota(jnp.int32, (SLOTS, LEAF), 1).astype(f32)
-            log_sum = lse[k, 0:1]
+            log_sum = lse[k]
             for c in range(4):
                 one = picks(table, c)
                 used = jnp.sum(jnp.where(one, 1.0, 0.0), axis=1, keepdims=True) > 0.5
@@ -505,62 +507,71 @@
             device_id={"label": dev}, device_id_type=MESH,
         )
 
+    def opposite():
+        s = column(3)
+        u = p.at[L.block(3, 0)]
+        u[...] = s(slice(None)).astype(u.dtype)
+        L.copy(u.at[LO], ah.at[0], 32, "a+")
+        L.copy(u.at[HI], ah.at[1], 33, "a-")
+
+    def beside_minus():
+        s = column(1)
+        u = p.at[L.block(1, 0)]
+        L.wait(ah.at[1], 33)
+        u[HI] = (s(HI) + ah[1].astype(f32)).astype(u.dtype)
+        u[LO] = s(LO).astype(u.dtype)
+        L.copy(u, af.at[1], 35, "a-")
+
+    def beside_plus():
+        s = column(2)
+        u = p.at[L.block(2, 0)]
+        L.wait(ah.at[0], 32)
+        u[LO] = (s(LO) + ah[0].astype(f32)).astype(u.dtype)
+        u[HI] = s(HI).astype(u.dtype)
+        L.copy(u, af.at[0], 34, "a+")
+
     part(0)
     pl.semaphore_wait(barrier, 34)
     slots(0)
     part(1)
-    for i in (3, 1, 2, 0):
-        far(i)
+    far(3)
+    far(1)
     part(2)
     part(3)
     mz[z] = ls[z]
     for off in (1, 2, 3):
         Z.copy(ls.at[lax.rem(z + off, 4)], mz.at[z], 41 + off, off)
-    slots(1)
     label_parts(0)
     Z.copy(lp.at[PAIRS[0], rows(2)], zh.at[0], 36, 1)
     near(3)
-    near(1)
     label_parts(2)
     Z.copy(lp.at[PAIRS[1], rows(2)], zh.at[1], 37, 3)
+    slots(1)
+    far(2)
+    near(1)
     for off in (1, 2, 3):
         L.wait(mz.at[lax.rem(z + 4 - off, 4)], 41 + off)
     mout[z, L.me] = mz[0] + mz[1] + mz[2] + mz[3]
     for k in peers:
         row_copy(k, L.me).start()
     slots(2)
+    opposite()
+    far(0)
+    near(2)
     L.wait(zh.at[0], 36)
-    zt[1, 0:2] = (lp[PAIRS[0], rows(1)].astype(f32) + zh[0].astype(f32)).astype(zt.dtype)
-    zt[1, 2:4] = lp[PAIRS[1], rows(1)]
-    Z.copy(zt.at[1], zf.at[0], 38, 1)
-    near(2)
+    lp[PAIRS[0], rows(1)] = (lp[PAIRS[0], rows(1)].astype(f32) + zh[0].astype(f32)).astype(bf16)
+    Z.copy(lp.at[:, rows(1)], zf.at[0], 38, 1)
+    L.wait(zh.at[1], 37)
+    lp[PAIRS[1], rows(3)] = (lp[PAIRS[1], rows(3)].astype(f32) + zh[1].astype(f32)).astype(bf16)
+    Z.copy(lp.at[:, rows(3)], zf.at[1], 39, 3)
+    beside_minus()
+    slots(3)
     near(0)
-    L.wait(zh.at[1], 37)
-    zt[0, 2:4] = (lp[PAIRS[1], rows(3)].astype(f32) + zh[1].astype(f32)).astype(zt.dtype)
-    zt[0, 0:2] = lp[PAIRS[0], rows(3)]
-    Z.copy(zt.at[0], zf.at[1], 39, 3)
-    slots(3)
+    beside_plus()
     for k in peers:
         row_copy(k, k).wait_recv()
     for off in (1, 2, 3):
         Z.copy(mout.at[z], mout.at[z], 44 + off, off)
-    s = column(3)
-    u = p.at[L.block(3, 0)]
-    u[...] = s(slice(None)).astype(u.dtype)
-    L.copy(u.at[LO], ah.at[0], 32, "a+")
-    L.copy(u.at[HI], ah.at[1], 33, "a-")
-    s = column(1)
-    u = p.at[L.block(1, 0)]
-    L.wait(ah.at[1], 33)
-    u[HI] = (s(HI) + ah[1].astype(f32)).astype(u.dtype)
-    u[LO] = s(LO).astype(u.dtype)
-    L.copy(u, af.at[1], 35, "a-")
-    s = column(2)
-    u = p.at[L.block(2, 0)]
-    L.wait(ah.at[0], 32)
-    u[LO] = (s(LO) + ah[0].astype(f32)).astype(u.dtype)
-    u[HI] = s(HI).astype(u.dtype)
-    L.copy(u, af.at[0], 34, "a+")
     L.wait(zf.at[0], 38)
     L.wait(zf.at[1], 39)
     label_out[...] = lp[:, rows(0)].astype(f32) + zf[0].astype(f32) + zf[1].astype(f32)
@@ -570,6 +581,9 @@
     out[...] = s(slice(None)) + af[0].astype(f32) + af[1].astype(f32)
     for off in (1, 2, 3):
         L.wait(mout.at[lax.rem(z + 4 - off, 4)], 44 + off)
+    for k in range(32):
+        for c in range(4):
+            matcher_out[4 * k + c : 4 * k + c + 1] = mout[c, k]
     for k in peers:
         row_copy(k, L.me).wait_send()
     L.drain()
@@ -584,10 +598,11 @@
     shape = jax.ShapeDtypeStruct
     return pl.pallas_call(
         backward_kernel,
-        out_shape=(shape((r, w), f32), shape((clusters, leaf // 4, w), f32), shape((4, n, 1, w), f32)),
+        out_shape=(shape((r, w), f32), shape((clusters, leaf // 4, w), f32), shape((4 * n, w), f32)),
         in_specs=[vmem] * 4 + [hbm] * 2,
         out_specs=(vmem,) * 3,
         scratch_shapes=[
+            pltpu.VMEM((4, n, 1, w), f32),
             pltpu.VMEM((2, 8, 4, SLOTS, leaf), f32),
             pltpu.VMEM((n, 4, SLOTS, w), bf16),
             pltpu.VMEM((n, 4, SLOTS, leaf), bf16),
@@ -601,7 +616,6 @@
             pltpu.VMEM((4, 2, r, w), bf16),
             pltpu.VMEM((2, r // 2, w), bf16),
             pltpu.VMEM((2, r, w), bf16),
-            pltpu.VMEM((2, clusters, leaf // 4, w), bf16),
             pltpu.VMEM((2, 2, leaf // 4, w), bf16),
             pltpu.VMEM((2, clusters, leaf // 4, w), bf16),
             pltpu.VMEM((4, 1, w), f32),
@@ -625,8 +639,9 @@
     ids = cluster_ids.reshape(n_label, q_dev, K).transpose(0, 2, 1)
     pos = positives.reshape(n_label, 1, q_dev)
     scores, received, info, lse, losses = forward(queries, labels, match, ids, pos)
-    query_grads, label_grads, rows = backward(labels, match, info, lse, scores, received)
-    matcher_grads = rows.transpose(1, 0, 2, 3).reshape(matcher.shape)
+    query_grads, label_grads, matcher_grads = backward(
+        labels, match, info, lse, scores, received
+    )
     return (losses.reshape(q_dev), query_grads, label_grads, matcher_grads)
 
 

time: 153 us -> 154 us (level)
    pallas_call x1, Pallas kernels: 68.5 us -> 71.5 us  [backward(): pl.pallas_call(backward_kernel, out_shape=(shape((r, w), f32), shape((clu...]
    unnamed x5 -> x6, local copies, waits for them, and re-layouts: 4.44 us -> 6.74 us
    pallas_call x1, Pallas kernels: 73.8 us -> 71.7 us  [forward(): pl.pallas_call(forward_kernel, out_shape=(shape((32, 4, SLOTS, LEAF), f32...]
where the time goes in v7:
time: 154 us
  Pallas kernels  143 us (93%)
  local copies, waits for them, and re-layouts  9.97 us (6%)
    pallas_call x1, Pallas kernels, forward(): pl.pallas_call(forward_kernel, out_shape=(shape((32, 4, SLOTS, LEAF), f32...  71.7 us
    pallas_call x1, Pallas kernels, backward(): pl.pallas_call(backward_kernel, out_shape=(shape((r, w), f32), shape((clu...  71.5 us
    unnamed x6, local copies, waits for them, and re-layouts  6.74 us

profile of v7, /device:TPU:1, one launch (start us, length us, event | category | flops | bytes accessed | tf_op | source)
XLA Modules:
  0.0 153.9 jit_solution(18320808901646850253)
XLA Ops:
  0.6 0.7 dynamic-slice_bitcast_fusion
  1.4 0.6 copy.10.match
  2.0 1.9 %copy.14 = s32[2,32,8,256]{3,2,0,1:T(8,128)} copy(s32[2,32,8,256]{3,2,1,0:T(8,128)} %bitcast.12) | data formatting | bytes 1048576 | tf_op jit(solution)/shard_map/reshape | solution.py:639
  3.9 71.7 %shard_map.84 = (f32[32,4,48,512]{3,2,1,0:T(8,128)}, bf16[32,4,48,768]{3,2,1,0:T(8,128)(2,1)}, f32[32,8,256]{2,1,0:T(8,128)}, f32[32,1,256]{2,1,0:T(1,128)}, f32[1,256]{1,0:T(1,128)}) custom-call(bf16[256,768]{1,0:T(8,128)(2,1)} %q_ref.1, bf16[4,512,768]{2,1,0:T(8,128)(2,1)} %labels.3, bf16[4,1,768]{2,1,0:T(2,128)(2,1)} %copy.10.match, ...), custom_call_target="tpu_custom_call" | custom-call | tf_op jit(solution)/shard_map/pallas_call | solution.py:305
  75.6 71.5 %shard_map.85 = (f32[256,768]{1,0:T(8,128)}, f32[4,128,768]{2,1,0:T(8,128)}, f32[128,768]{1,0:T(8,128)}) custom-call(bf16[4,512,768]{2,1,0:T(8,128)(2,1)} %labels.3, bf16[4,1,768]{2,1,0:T(2,128)(2,1)} %copy.10.match, f32[32,8,256]{2,1,0:T(8,128)} %get-tuple-element.13.info, f32[32,1,256]{2,1,0:T(1,128)} %get-tuple-element.14.lse, ...), custom_call_target="tpu_custom_call" | custom-call | tf_op jit(solution)/shard_map/pallas_call | solution.py:599
  147.1 0.0 copy-start
  147.1 1.2 copy.19
  148.4 2.1 %copy.20 = f32[256,768]{1,0:T(8,128)} copy(f32[256,768]{1,0:T(8,128)} %get-tuple-element.25) | data formatting | bytes 1572864
  150.4 2.7 %copy.21 = f32[4,128,768]{2,1,0:T(8,128)} copy(f32[4,128,768]{2,1,0:T(8,128)} %get-tuple-element.26) | data formatting | bytes 3145728
  153.1 0.0 copy-done
  153.1 0.7 copy.22
Async XLA Ops:
  147.1 6.0 %copy-start = (f32[128,768]{1,0:T(8,128)S(1)}, f32[128,768]{1,0:T(8,128)}, u32[]{:S(2)}) copy-start(f32[128,768]{1,0:T(8,128)} %get-tuple-element.27) | copy-start | bytes 1179652

commit v8 on v6

--- a/solution.py
+++ b/solution.py
@@ -26,6 +26,15 @@
     return (y * 4 + x) * 2 + core
 
 OFF = (0, 3, 1, 2)
+
+def in_pairs(count, step):
+    def two(n, carry):
+        step(2 * n, 0)
+        step(2 * n + 1, 0)
+        return carry
+
+    lax.fori_loop(0, count // 2, two, 0)
+
 
 class Links:
     def __init__(self, send, recv):
@@ -66,10 +75,10 @@
 
 SLOTS = 48
 TURNS = (
-    ((0, 0), (1, 0), (2, 0), (0, 1)),
-    ((0, 2), (3, 0), (0, 3), (1, 1)),
-    ((1, 2), (2, 1), (2, 2), (1, 3)),
-    ((3, 1), (3, 2), (2, 3), (3, 3)),
+    ((0, 0), (1, 0), (2, 0), (0, 1), (0, 2)),
+    ((3, 0), (0, 3), (1, 1), (1, 2)),
+    ((2, 1), (2, 2), (1, 3), (3, 1), (3, 2)),
+    ((2, 3), (3, 3)),
 )
 
 
@@ -127,7 +136,7 @@
         info[s] = slot_tables(ids_ref[s] - first, pos_ref[s])
         return carry
 
-    lax.fori_loop(0, 32, tables, 0)
+    in_pairs(32, tables)
 
     def side_a(i):
         k = L.block(i, 0)
@@ -166,13 +175,15 @@
 
     def work(turn, middle):
         members = TURNS[turn]
+        size = len(members)
+        base = 2 * sum(len(t) for t in TURNS[:turn])
         for i, j in members:
             L.wait(g.at[L.partner_block(i, j)], 20 + 4 * i + j)
         code_a = sum(OFF[i] << (2 * n) for n, (i, j) in enumerate(members))
         code_b = sum(OFF[j] << (2 * n) for n, (i, j) in enumerate(members))
 
         def block_of(n):
-            other, m = n // 4, lax.rem(n, 4)
+            other, m = n // size, lax.rem(n, size)
             core = L.core + other - 2 * L.core * other
             da = lax.rem(lax.shift_right_logical(jnp.int32(code_a), 2 * m), 4)
             db = lax.rem(lax.shift_right_logical(jnp.int32(code_b), 2 * m), 4)
@@ -190,7 +201,7 @@
             rec[s] = rows.astype(jnp.bfloat16).reshape(4, SLOTS, rows.shape[1])
             return carry
 
-        lax.fori_loop(0, 8, pick, 0)
+        in_pairs(2 * size, pick)
         middle()
 
         def score(c, carry):
@@ -228,13 +239,12 @@
                     jnp.where(one, total * jnp.exp(jnp.where(one, top - best, 0.0)), 0.0), axis=0, keepdims=True
                 )
                 chosen += jnp.sum(jnp.where(one, picked, 0.0), axis=0, keepdims=True)
-            line = lax.broadcasted_iota(jnp.int32, (8, table.shape[1]), 0)
-            st[s] = jnp.where(line == 0, best, jnp.where(line == 1, spread, chosen))
+            st[s] = jnp.concatenate([best, spread, chosen], axis=1)
             return carry
 
-        lax.fori_loop(0, 8, stat, 0)
+        in_pairs(2 * size, stat)
         for m, k in enumerate(blocks):
-            n = 8 * turn + m
+            n = base + m
             pltpu.make_async_copy(scores.at[k], scores_out.at[k], out_sem.at[2 * n]).start()
             pltpu.make_async_copy(rec.at[k], rec_out.at[k], out_sem.at[2 * n + 1]).start()
             if n == 0:
@@ -249,12 +259,12 @@
     side_a(2)
     side_b(0)
     order = work(0, far_a)
+    far_b(0)
     side_b(1)
-    far_b(0)
     order += work(1, lambda: side_b(2))
     far_b(1)
-    order += work(2, lambda: side_b(3))
-    far_b(2)
+    side_b(3)
+    order += work(2, lambda: far_b(2))
     far_b(3)
     order += work(3, lambda: None)
     sr[own] = st[own]
@@ -267,13 +277,14 @@
 
     for k in peers:
         stat_copy(k, True).wait_recv()
-    best = jnp.max(sr[:, 0:1, :], axis=0)
-    lines = sr[...]
-    spread = jnp.sum(lines[:, 1:2, :] * jnp.exp(lines[:, 0:1, :] - best[None]), axis=0)
-    chosen = jnp.sum(lines[:, 2:3, :], axis=0)
+    q_dev = q_ref.shape[0]
+    tops = sr[:, :, 0:q_dev]
+    best = jnp.max(tops, axis=0)
+    spread = jnp.sum(sr[:, :, q_dev : 2 * q_dev] * jnp.exp(tops - best[None]), axis=0)
+    chosen = jnp.sum(sr[:, :, 2 * q_dev : 3 * q_dev], axis=0)
     value = best + jnp.log(spread)
     losses[...] = value - chosen
-    lse[own] = jnp.broadcast_to(value, lse.shape[1:])
+    lse[own] = value
 
     def lse_copy(dev, row):
         return pltpu.make_async_remote_copy(
@@ -306,7 +317,7 @@
             shape((32, 4, SLOTS, LEAF), f32),
             shape((32, 4, SLOTS, width), bf16),
             shape((32, 8, q_dev), f32),
-            shape((32, 8, q_dev), f32),
+            shape((32, 1, q_dev), f32),
             shape((1, q_dev), f32),
         ),
         in_specs=[vmem] * 5,
@@ -315,8 +326,8 @@
             pltpu.VMEM((32, q_dev, width), bf16),
             pltpu.VMEM((32, 4, SLOTS, LEAF), f32),
             pltpu.VMEM((32, 4, SLOTS, width), bf16),
-            pltpu.VMEM((32, 8, q_dev), f32),
-            pltpu.VMEM((32, 8, q_dev), f32),
+            pltpu.VMEM((32, 1, 3 * q_dev), f32),
+            pltpu.VMEM((32, 1, 3 * q_dev), f32),
             dma((36,)), dma((36,)), dma((32,)), dma((32,)), dma((32,)), dma((32,)), dma((64,)),
         ],
         compiler_params=pltpu.CompilerParams(
@@ -350,7 +361,7 @@
 
 
 def backward_kernel(labels, match, info, lse, scores_hbm, rec_hbm, out, label_out, mout,
-                    stage, rec, delta, coef, grads, p, lp, ls, pr, bh, bf, ah, af, zt, zh, zf, mz,
+                    stage, rec, delta, coef, grads, p, lp, ls, pr, bh, bf, ah, af, zh, zf, mz,
                     send, recv, m_recv, in_sem):
     L = Links(send, recv)
     Z = Column(L)
@@ -406,7 +417,7 @@
             k = block_of(t, n)
             table = info[k]
             leaf = lax.broadcasted_iota(jnp.int32, (SLOTS, LEAF), 1).astype(f32)
-            log_sum = lse[k, 0:1]
+            log_sum = lse[k]
             for c in range(4):
                 one = picks(table, c)
                 used = jnp.sum(jnp.where(one, 1.0, 0.0), axis=1, keepdims=True) > 0.5
@@ -420,7 +431,7 @@
                 ls[c] += jnp.sum(total.astype(f32) * rec[k, c].astype(f32), axis=0, keepdims=True)
             return carry
 
-        lax.fori_loop(0, 8, step, 0)
+        in_pairs(8, step)
         if t < 2:
             for c in load_scores(t + 2):
                 c.start()
@@ -445,7 +456,7 @@
             p[k] = val.astype(bf16)
             return carry
 
-        lax.fori_loop(0, 8, back, 0)
+        in_pairs(8, back)
         for i, j in BACK_TURNS[t]:
             L.copy(p.at[L.partner_block(i, j)], pr.at[4 * i + j], 4 * i + j, "p")
 
@@ -530,15 +541,13 @@
         row_copy(k, L.me).start()
     slots(2)
     L.wait(zh.at[0], 36)
-    zt[1, 0:2] = (lp[PAIRS[0], rows(1)].astype(f32) + zh[0].astype(f32)).astype(zt.dtype)
-    zt[1, 2:4] = lp[PAIRS[1], rows(1)]
-    Z.copy(zt.at[1], zf.at[0], 38, 1)
+    lp[PAIRS[0], rows(1)] = (lp[PAIRS[0], rows(1)].astype(f32) + zh[0].astype(f32)).astype(bf16)
+    Z.copy(lp.at[:, rows(1)], zf.at[0], 38, 1)
     near(2)
     near(0)
     L.wait(zh.at[1], 37)
-    zt[0, 2:4] = (lp[PAIRS[1], rows(3)].astype(f32) + zh[1].astype(f32)).astype(zt.dtype)
-    zt[0, 0:2] = lp[PAIRS[0], rows(3)]
-    Z.copy(zt.at[0], zf.at[1], 39, 3)
+    lp[PAIRS[1], rows(3)] = (lp[PAIRS[1], rows(3)].astype(f32) + zh[1].astype(f32)).astype(bf16)
+    Z.copy(lp.at[:, rows(3)], zf.at[1], 39, 3)
     slots(3)
     for k in peers:
         row_copy(k, k).wait_recv()
@@ -601,7 +610,6 @@
             pltpu.VMEM((4, 2, r, w), bf16),
             pltpu.VMEM((2, r // 2, w), bf16),
             pltpu.VMEM((2, r, w), bf16),
-            pltpu.VMEM((2, clusters, leaf // 4, w), bf16),
             pltpu.VMEM((2, 2, leaf // 4, w), bf16),
             pltpu.VMEM((2, clusters, leaf // 4, w), bf16),
             pltpu.VMEM((4, 1, w), f32),

time: 153 us -> 145 us (0.948)
  Pallas kernels: 142 us -> 135 us
    pallas_call x1, Pallas kernels: 73.8 us -> 68.8 us  [forward(): pl.pallas_call(forward_kernel, out_shape=(shape((32, 4, SLOTS, LEAF), f32...]
    pallas_call x1, Pallas kernels: 68.5 us -> 65.8 us  [backward(): pl.pallas_call(backward_kernel, out_shape=(shape((r, w), f32), shape((clu...]
where the time goes in v8:
time: 145 us
  Pallas kernels  135 us (93%)
  local copies, waits for them, and re-layouts  9.87 us (7%)
    pallas_call x1, Pallas kernels, forward(): pl.pallas_call(forward_kernel, out_shape=(shape((32, 4, SLOTS, LEAF), f32...  68.8 us
    pallas_call x1, Pallas kernels, backward(): pl.pallas_call(backward_kernel, out_shape=(shape((r, w), f32), shape((clu...  65.8 us
    unnamed x5, local copies, waits for them, and re-layouts  4.39 us

profile of v8, /device:TPU:1, one launch (start us, length us, event | category | flops | bytes accessed | tf_op | source)
XLA Modules:
  0.0 145.1 jit_solution(13838142435630817767)
XLA Ops:
  0.6 0.7 dynamic-slice_bitcast_fusion
  1.4 0.6 copy.10.match
  2.0 1.9 %copy.15 = s32[2,32,8,256]{3,2,0,1:T(8,128)} copy(s32[2,32,8,256]{3,2,1,0:T(8,128)} %bitcast.15) | data formatting | bytes 1048576 | tf_op jit(solution)/shard_map/reshape | solution.py:633
  3.9 68.8 %shard_map.84 = (f32[32,4,48,512]{3,2,1,0:T(8,128)}, bf16[32,4,48,768]{3,2,1,0:T(8,128)(2,1)}, f32[32,8,256]{2,1,0:T(8,128)}, f32[32,1,256]{2,1,0:T(1,128)}, f32[1,256]{1,0:T(1,128)}) custom-call(bf16[256,768]{1,0:T(8,128)(2,1)} %q_ref.1, bf16[4,512,768]{2,1,0:T(8,128)(2,1)} %labels.3, bf16[4,1,768]{2,1,0:T(2,128)(2,1)} %copy.10.match, ...), custom_call_target="tpu_custom_call" | custom-call | tf_op jit(solution)/shard_map/pallas_call | solution.py:314
  72.7 65.8 %shard_map.85 = (f32[256,768]{1,0:T(8,128)}, f32[4,128,768]{2,1,0:T(8,128)}, f32[4,32,1,768]{3,2,1,0:T(1,128)}) custom-call(bf16[4,512,768]{2,1,0:T(8,128)(2,1)} %labels.3, bf16[4,1,768]{2,1,0:T(2,128)(2,1)} %copy.10.match, f32[32,8,256]{2,1,0:T(8,128)} %get-tuple-element.13.info, f32[32,1,256]{2,1,0:T(1,128)} %get-tuple-element.14.lse, ...), custom_call_target="tpu_custom_call" | custom-call | tf_op jit(solution)/shard_map/pallas_call | solution.py:594
  138.5 0.0 copy-start
  138.5 1.4 copy.12
  139.9 0.9 reshape.27
  140.7 1.2 copy.19
  141.9 2.1 %copy.20 = f32[256,768]{1,0:T(8,128)} copy(f32[256,768]{1,0:T(8,128)} %get-tuple-element.25) | data formatting | bytes 1572864
  144.0 0.0 copy-done
  144.0 1.1 copy.21
Async XLA Ops:
  138.5 5.5 %copy-start = (f32[4,128,768]{2,1,0:T(8,128)S(1)}, f32[4,128,768]{2,1,0:T(8,128)}, u32[]{:S(2)}) copy-start(f32[4,128,768]{2,1,0:T(8,128)} %get-tuple-element.26) | copy-start | bytes 4718596
